TPU v7x, 32 devices: a whole 2x2x4 slice. The times are simulated.
32 devices in a mesh: tm: 4 (over y, x), row: 8 (over z, core).
Axes of the slice: x: 2, y: 2, z: 4, core: 2. Of those that a mesh axis runs over, the one named last changes fastest.
Arguments:
- coupling: float32 [4, 8192, 8192], P('tm', 'row'), may hold values from -0.0625 to 0.0625
- damping: float32 [4, 8192], P('tm', 'row'), may hold values from 0.5 to 3
- forcing: float32 [4, 8, 8192], P('tm', None, 'row'), may hold values from -6 to 6
- initial: float32 [8, 8192], P(None, 'row'), may hold values from -6 to 6
- counts: int32 [4], P('tm'), may hold values from 1 to 8
Outputs:
- states: float32 [4, 8, 8192], P('tm', None, 'row')
All inputs are finite; a program needn't handle non-finite values.
Results may differ from a plain program's by a relative error of at most 0.00013.
Values sent between devices are 32-bit elements; how exact they have to be, the bound alone decides.
No kernel may reach another device: no remote copies, remote signals or barrier semaphores. Data moves between devices by JAX's collectives and lax.ppermute only.
A program may use at most 128 MiB of HBM per device.

v0:
```python
import jax
import jax.numpy as jnp
from jax import lax
from jax.sharding import PartitionSpec as P

KRYLOV = 2


time_step = 0.125
epsilon = 1e-06
squarings = 5
taylor_terms = 12
highest = lax.Precision.HIGHEST


def passed_along(array, axis, by):
    size = lax.axis_size(axis)
    pairs = [(i, i + by) for i in range(size) if 0 <= i + by < size]
    return lax.ppermute(array, axis, pairs)


def matrix_exponential(matrix):
    scaled = matrix / 2.0**squarings
    dimension = matrix.shape[-1]
    identity = jnp.broadcast_to(jnp.eye(dimension, dtype=jnp.float32), matrix.shape)
    result = identity
    for degree in range(taylor_terms, 0, -1):
        result = identity + jnp.einsum("bij,bjk->bik", scaled, result, precision=highest) / degree
    for repeat in range(squarings):
        result = jnp.einsum("bij,bjk->bik", result, result, precision=highest)
    return result


def exponent_block(hessenberg, step_size):
    members = hessenberg.shape[0]
    augmented = jnp.zeros((members, KRYLOV + 1, KRYLOV + 1), jnp.float32)
    augmented = augmented.at[:, :KRYLOV, :KRYLOV].set(step_size * hessenberg)
    augmented = augmented.at[:, 0, KRYLOV].set(1.0)
    return matrix_exponential(augmented)


def rows_product(vectors, local_coupling):
    return lax.dot_general(
        vectors,
        local_coupling,
        (((1,), (1,)), ((), ())),
        precision=highest,
        preferred_element_type=jnp.float32,
    )


def combine_basis(krylov_basis, coefficients):
    return jnp.einsum("kbn,bk->bn", krylov_basis, coefficients, precision=highest)


def whole_arnoldi(vectors, local_coupling, local_damping, row_offset):
    members = vectors.shape[0]
    extent = vectors.shape[1]
    rows_local = local_coupling.shape[0]
    start_norm = jnp.sqrt(jnp.sum(vectors * vectors, axis=1) + epsilon)
    krylov_basis = (
        jnp.zeros((KRYLOV, members, extent), jnp.float32).at[0].set(vectors / start_norm[:, None])
    )
    hessenberg = jnp.zeros((members, KRYLOV, KRYLOV), jnp.float32)
    for column in range(KRYLOV):
        current = krylov_basis[column]
        own_rows = lax.dynamic_slice_in_dim(current, row_offset, rows_local, 1)
        applied_rows = rows_product(current, local_coupling) - local_damping * own_rows
        applied = lax.all_gather(applied_rows, "row", axis=1, tiled=True)
        weights = jnp.einsum("kbn,bn->kb", krylov_basis, applied, precision=highest)
        applied = applied - jnp.einsum("kb,kbn->bn", weights, krylov_basis, precision=highest)
        hessenberg = hessenberg.at[:, :, column].set(weights.T)
        if column + 1 < KRYLOV:
            length = jnp.sqrt(jnp.sum(applied * applied, axis=1) + epsilon)
            krylov_basis = krylov_basis.at[column + 1].set(applied / length[:, None])
            hessenberg = hessenberg.at[:, column + 1, column].set(length)
    return (start_norm, krylov_basis, hessenberg)


def on_device(coupling, damping, forcing, initial, counts):
    local_coupling = coupling[0]
    local_damping = damping[0]
    local_forcing = forcing[0]
    rows_local = local_coupling.shape[0]
    step_size = counts[0].astype(jnp.float32) * time_step
    slab_index = lax.axis_index("tm")
    row_offset = lax.axis_index("row") * rows_local
    sections = lax.axis_size("tm")

    def run_arnoldi(vectors):
        outcome = whole_arnoldi(vectors, local_coupling, local_damping, row_offset)
        return outcome

    def carried_term(norms, krylov_basis, hessenberg):
        block = exponent_block(hessenberg, step_size)
        return combine_basis(krylov_basis, norms[:, None] * block[:, :KRYLOV, 0])

    forcing_vectors, incoming = (
        lax.all_gather(local_forcing, "row", axis=1, tiled=True),
        lax.all_gather(initial, "row", axis=1, tiled=True),
    )
    forcing_norm, forcing_basis, forcing_hessenberg = run_arnoldi(forcing_vectors)
    block = exponent_block(forcing_hessenberg, step_size)
    local_part = combine_basis(
        forcing_basis, (step_size * forcing_norm)[:, None] * block[:, :KRYLOV, KRYLOV]
    )
    carried_norm, carried_basis, carried_hessenberg = run_arnoldi(incoming)
    section_zero = carried_term(carried_norm, carried_basis, carried_hessenberg) + local_part
    result = jnp.zeros_like(incoming)
    for section in range(sections):
        if section == 0:
            outgoing = section_zero
        else:
            carried_norm, carried_basis, carried_hessenberg = run_arnoldi(incoming)
            outgoing = carried_term(carried_norm, carried_basis, carried_hessenberg) + local_part
        result = jnp.where(slab_index == section, outgoing, result)
        if section + 1 < sections:
            incoming = passed_along(outgoing, "tm", 1)
    result = lax.dynamic_slice_in_dim(result, row_offset, rows_local, 1)
    return result[None]


def solution(mesh):
    placed = (P("tm", "row", None), P("tm", "row"), P("tm", None, "row"), P(None, "row"), P("tm"))
    return jax.shard_map(
        on_device, mesh=mesh, in_specs=placed, out_specs=P("tm", None, "row"), check_vma=False
    )
```

profile of v0, /device:TPU:0, one launch (start us, length us, event | category | flops | bytes accessed | tf_op | source)
XLA Modules:
  0.0 619.0 jit_solution(6166676767222239010)
XLA Ops:
  0.0 16.2 %all_gather.36 = f32[8,8192]{1,0:T(8,128)S(1)} all-gather(f32[8,1024]{1,0:T(8,128)} %param.78), channel_id=1, replica_groups=mesh['tm'=4,'row'=8] {'row'}, dimensions={1}, use_global_device_ids=true | all-gather | bytes 294912 | tf_op jit(solution)/shard_map/all_gather | solution.py:100
  17.3 14.4 %all-gather = f32[1,8,8192]{2,1,0:T(8,128)S(1)} all-gather(f32[1,8,1024]{2,1,0:T(8,128)} %param.77), channel_id=2, replica_groups=mesh['tm'=4,'row'=8] {'row'}, dimensions={2}, use_global_device_ids=true | all-gather | bytes 294912 | tf_op jit(solution)/shard_map/all_gather | solution.py:99
  32.1 30.8 %fusion.20 = f32[8,1024]{1,0:T(8,128)S(1)} fusion(f32[8,8192]{1,0:T(8,128)S(1)} %broadcast_divide_fusion.8, f32[1,1024,8192]{2,1,0:T(8,128)} %param.75, s32[]{:T(128)S(6)} %select_n.40, f32[1024]{0:T(1024)} %bitcast.407), kind=kOutput, calls=%fused_computation.20 | convolution fusion | flops 805322752 | bytes 33886212 | tf_op jit(solution)/shard_map/dot_general | solution.py:43
  62.9 14.4 %all_gather.37 = f32[8,8192]{1,0:T(8,128)S(1)} all-gather(f32[8,1024]{1,0:T(8,128)S(1)} %fusion.20), channel_id=1, replica_groups=mesh['tm'=4,'row'=8] {'row'}, dimensions={1}, use_global_device_ids=true | all-gather | bytes 294912 | tf_op jit(solution)/shard_map/all_gather | solution.py:69
  77.6 4.7 fusion.123
  84.8 29.8 %fusion.23 = f32[8,1024]{1,0:T(8,128)S(1)} fusion(f32[8,8192]{1,0:T(8,128)S(1)} %broadcast_divide_fusion.7, f32[1,1024,8192]{2,1,0:T(8,128)} %param.75, s32[]{:T(128)S(6)} %select_n.40, f32[1024]{0:T(1024)S(1)} %bitcast.408), kind=kOutput, calls=%fused_computation.21 | convolution fusion | flops 805322752 | bytes 33886212 | tf_op jit(solution)/shard_map/dot_general | solution.py:43
  114.6 14.5 %all_gather.38 = f32[8,8192]{1,0:T(8,128)S(1)} all-gather(f32[8,1024]{1,0:T(8,128)S(1)} %fusion.23), channel_id=1, replica_groups=mesh['tm'=4,'row'=8] {'row'}, dimensions={1}, use_global_device_ids=true | all-gather | bytes 294912 | tf_op jit(solution)/shard_map/all_gather | solution.py:69
  129.1 4.9 fusion.143
  134.1 29.8 %fusion.26 = f32[8,1024]{1,0:T(8,128)S(1)} fusion(f32[8,8192]{1,0:T(8,128)S(1)} %bitcast_divide_fusion, f32[1,1024,8192]{2,1,0:T(8,128)} %param.75, s32[]{:T(128)S(6)} %select_n.40, f32[1024]{0:T(1024)S(1)} %bitcast.409), kind=kOutput, calls=%fused_computation.22 | convolution fusion | flops 805322752 | bytes 33886212 | tf_op jit(solution)/shard_map/dot_general | solution.py:43
  163.9 14.7 %all_gather.40 = f32[8,8192]{1,0:T(8,128)S(1)} all-gather(f32[8,1024]{1,0:T(8,128)S(1)} %fusion.26), channel_id=1, replica_groups=mesh['tm'=4,'row'=8] {'row'}, dimensions={1}, use_global_device_ids=true | all-gather | bytes 294912 | tf_op jit(solution)/shard_map/all_gather | solution.py:69
  178.8 4.7 fusion.119
  186.1 29.8 %fusion.29 = f32[8,1024]{1,0:T(8,128)S(1)} fusion(f32[8,8192]{1,0:T(8,128)S(1)} %broadcast_divide_fusion.6, f32[1,1024,8192]{2,1,0:T(8,128)} %param.75, s32[]{:T(128)S(6)} %select_n.40, f32[1024]{0:T(1024)S(1)} %bitcast.410), kind=kOutput, calls=%fused_computation.23 | convolution fusion | flops 805322752 | bytes 33886212 | tf_op jit(solution)/shard_map/dot_general | solution.py:43
  215.9 14.4 %all_gather.41 = f32[8,8192]{1,0:T(8,128)S(1)} all-gather(f32[8,1024]{1,0:T(8,128)S(1)} %fusion.29), channel_id=1, replica_groups=mesh['tm'=4,'row'=8] {'row'}, dimensions={1}, use_global_device_ids=true | all-gather | bytes 294912 | tf_op jit(solution)/shard_map/all_gather | solution.py:69
  230.3 4.9 fusion.139
  236.8 1.9 broadcast_select_fusion.3
  238.7 1.9 broadcast_select_fusion.4
  245.7 2.1 fusion.137
  252.7 2.1 fusion.141
  255.1 3.4 collective-permute-start
  258.5 6.0 collective-permute-done
  264.8 29.8 %fusion.32 = f32[8,1024]{1,0:T(8,128)S(1)} fusion(f32[8,8192]{1,0:T(8,128)S(1)} %broadcast_divide_fusion.5, f32[1,1024,8192]{2,1,0:T(8,128)} %param.75, s32[]{:T(128)S(6)} %select_n.40, f32[1024]{0:T(1024)S(1)} %bitcast.411), kind=kOutput, calls=%fused_computation.24 | convolution fusion | flops 805322752 | bytes 33886212 | tf_op jit(solution)/shard_map/dot_general | solution.py:43
  294.6 14.7 %all_gather.42 = f32[8,8192]{1,0:T(8,128)S(1)} all-gather(f32[8,1024]{1,0:T(8,128)S(1)} %fusion.32), channel_id=1, replica_groups=mesh['tm'=4,'row'=8] {'row'}, dimensions={1}, use_global_device_ids=true | all-gather | bytes 294912 | tf_op jit(solution)/shard_map/all_gather | solution.py:69
  309.7 4.7 fusion.115
  317.0 29.8 %fusion.35 = f32[8,1024]{1,0:T(8,128)S(1)} fusion(f32[8,8192]{1,0:T(8,128)S(1)} %broadcast_divide_fusion.4, f32[1,1024,8192]{2,1,0:T(8,128)} %param.75, s32[]{:T(128)S(6)} %select_n.40, f32[1024]{0:T(1024)S(1)} %bitcast.412), kind=kOutput, calls=%fused_computation.25 | convolution fusion | flops 805322752 | bytes 33886212 | tf_op jit(solution)/shard_map/dot_general | solution.py:43
  346.8 14.4 %all_gather.43 = f32[8,8192]{1,0:T(8,128)S(1)} all-gather(f32[8,1024]{1,0:T(8,128)S(1)} %fusion.35), channel_id=1, replica_groups=mesh['tm'=4,'row'=8] {'row'}, dimensions={1}, use_global_device_ids=true | all-gather | bytes 294912 | tf_op jit(solution)/shard_map/all_gather | solution.py:69
  361.2 4.9 fusion.135
  366.3 1.9 broadcast_select_fusion.2
  373.1 2.1 fusion.133
  375.5 4.4 collective-permute-start.1
  379.9 6.0 collective-permute-done.1
  386.2 29.8 %fusion.38 = f32[8,1024]{1,0:T(8,128)S(1)} fusion(f32[8,8192]{1,0:T(8,128)S(1)} %broadcast_divide_fusion.3, f32[1,1024,8192]{2,1,0:T(8,128)} %param.75, s32[]{:T(128)S(6)} %select_n.40, f32[1024]{0:T(1024)S(1)} %bitcast.413), kind=kOutput, calls=%fused_computation.26 | convolution fusion | flops 805322752 | bytes 33886212 | tf_op jit(solution)/shard_map/dot_general | solution.py:43
  416.0 14.7 %all_gather.44 = f32[8,8192]{1,0:T(8,128)S(1)} all-gather(f32[8,1024]{1,0:T(8,128)S(1)} %fusion.38), channel_id=1, replica_groups=mesh['tm'=4,'row'=8] {'row'}, dimensions={1}, use_global_device_ids=true | all-gather | bytes 294912 | tf_op jit(solution)/shard_map/all_gather | solution.py:69
  431.1 4.7 fusion.111
  438.3 29.8 %fusion.41 = f32[8,1024]{1,0:T(8,128)S(1)} fusion(f32[8,8192]{1,0:T(8,128)S(1)} %broadcast_divide_fusion.2, f32[1,1024,8192]{2,1,0:T(8,128)} %param.75, s32[]{:T(128)S(6)} %select_n.40, f32[1024]{0:T(1024)S(1)} %bitcast.414), kind=kOutput, calls=%fused_computation.27 | convolution fusion | flops 805322752 | bytes 33886212 | tf_op jit(solution)/shard_map/dot_general | solution.py:43
  468.2 14.4 %all_gather.45 = f32[8,8192]{1,0:T(8,128)S(1)} all-gather(f32[8,1024]{1,0:T(8,128)S(1)} %fusion.41), channel_id=1, replica_groups=mesh['tm'=4,'row'=8] {'row'}, dimensions={1}, use_global_device_ids=true | all-gather | bytes 294912 | tf_op jit(solution)/shard_map/all_gather | solution.py:69
  482.5 4.9 fusion.131
  487.6 1.9 broadcast_select_fusion.1
  494.5 2.1 fusion.129
  496.8 4.4 collective-permute-start.2
  501.4 5.9 collective-permute-done.2
  507.6 29.8 %fusion.44 = f32[8,1024]{1,0:T(8,128)S(1)} fusion(f32[8,8192]{1,0:T(8,128)S(1)} %broadcast_divide_fusion.1, f32[1,1024,8192]{2,1,0:T(8,128)} %param.75, s32[]{:T(128)S(6)} %select_n.40, f32[1024]{0:T(1024)S(1)} %bitcast.415), kind=kOutput, calls=%fused_computation.28 | convolution fusion | flops 805322752 | bytes 33886212 | tf_op jit(solution)/shard_map/dot_general | solution.py:43
  537.4 14.5 %all_gather.46 = f32[8,8192]{1,0:T(8,128)S(1)} all-gather(f32[8,1024]{1,0:T(8,128)S(1)} %fusion.44), channel_id=1, replica_groups=mesh['tm'=4,'row'=8] {'row'}, dimensions={1}, use_global_device_ids=true | all-gather | bytes 294912 | tf_op jit(solution)/shard_map/all_gather | solution.py:69
  552.3 4.7 fusion.107
  559.5 29.8 %fusion.47 = f32[8,1024]{1,0:T(8,128)S(1)} fusion(f32[8,8192]{1,0:T(8,128)S(1)} %broadcast_divide_fusion, f32[1,1024,8192]{2,1,0:T(8,128)} %param.75, s32[]{:T(128)S(6)} %select_n.40, f32[1024]{0:T(1024)S(1)} %bitcast.416), kind=kOutput, calls=%fused_computation.29 | convolution fusion | flops 805322752 | bytes 33886212 | tf_op jit(solution)/shard_map/dot_general | solution.py:43
  589.3 14.4 %all_gather.47 = f32[8,8192]{1,0:T(8,128)S(1)} all-gather(f32[8,1024]{1,0:T(8,128)S(1)} %fusion.47), channel_id=1, replica_groups=mesh['tm'=4,'row'=8] {'row'}, dimensions={1}, use_global_device_ids=true | all-gather | bytes 294912 | tf_op jit(solution)/shard_map/all_gather | solution.py:69
  603.8 4.9 fusion.127
  608.8 1.9 broadcast_select_fusion
  615.7 2.1 fusion.125
  (218 shorter events, 44.0 us)
Async XLA Ops:
  0.0 84.8 %copy-start = (f32[1,1024]{1,0:T(1,128)S(1)}, f32[1,1024]{1,0:T(1,128)}, u32[]{:S(2)}) copy-start(f32[1,1024]{1,0:T(1,128)} %param.76) | copy-start | bytes 12292
  134.1 102.0 %copy-start.1 = (s32[3]{0:T(128)S(1)}, s32[3]{0:T(128)}, u32[]{:S(2)}) copy-start(s32[3]{0:T(128)} %constant.860.clone.1) | copy-start | bytes 40
  255.1 9.5 %collective-permute-start = (f32[8,8192]{1,0:T(8,128)S(1)}, f32[8,8192]{1,0:T(8,128)S(1)}, u32[]{:S(2)}, u32[]{:S(2)}) collective-permute-start(f32[8,8192]{1,0:T(8,128)S(1)} %bitcast_add_fusion.2), channel_id=1, source_target_pairs={{0,8},{8,16},{16,24},{1,9},{9,17},{17,25},{2,10},{10,18},{18,26},{... | collective-permute-start | bytes 786440 | tf_op jit(solution)/shard_map/ppermute | solution.py:19
  375.5 10.5 %collective-permute-start.1 = (f32[8,8192]{1,0:T(8,128)S(1)}, f32[8,8192]{1,0:T(8,128)S(1)}, u32[]{:S(2)}, u32[]{:S(2)}) collective-permute-start(f32[8,8192]{1,0:T(8,128)S(1)} %bitcast_add_fusion.1), channel_id=1, source_target_pairs={{0,8},{8,16},{16,24},{1,9},{9,17},{17,25},{2,10},{10,18},{18,26},{... | collective-permute-start | bytes 786440 | tf_op jit(solution)/shard_map/ppermute | solution.py:19
  496.8 10.5 %collective-permute-start.2 = (f32[8,8192]{1,0:T(8,128)S(1)}, f32[8,8192]{1,0:T(8,128)S(1)}, u32[]{:S(2)}, u32[]{:S(2)}) collective-permute-start(f32[8,8192]{1,0:T(8,128)S(1)} %bitcast_add_fusion), channel_id=1, source_target_pairs={{0,8},{8,16},{16,24},{1,9},{9,17},{17,25},{2,10},{10,18},{18,26},{... | collective-permute-start | bytes 786440 | tf_op jit(solution)/shard_map/ppermute | solution.py:19
where the time goes:
time: 628 us; the launch traced here: 619 us
  matrix products  383 us (61%)
  blocking collectives  176 us (28%)
  waiting for transfers between devices  17.9 us (3%)
  other arithmetic  16.1 us (3%)
  starting transfers between devices  12.2 us (2%)
  local copies, waits for them, and re-layouts  11.7 us (2%)
    dot_general x10, matrix products, rows_product(): lax.dot_general(vectors, local_coupling, (((1,), (1,)), ((), ())), precis...  299 us
    all_gather x10, blocking collectives, whole_arnoldi(): applied = lax.all_gather(applied_rows, 'row', axis=1, tiled=True)  145 us
    dot_general x10, matrix products, whole_arnoldi(): weights = jnp.einsum('kbn,bn->kb', krylov_basis, applied, precision=highest)  48.1 us
    ppermute x3, waiting for transfers between devices, passed_along(): return lax.ppermute(array, axis, pairs)  17.9 us
    all_gather x1, blocking collectives, on_device(): lax.all_gather(initial, 'row', axis=1, tiled=True)  16.2 us
    all_gather x1, blocking collectives, on_device(): lax.all_gather(local_forcing, 'row', axis=1, tiled=True)  14.4 us
  transfers between devices with their start and end apart: 3, of which 3 were waited for; matrix products, arithmetic and copies ran while one was open for 0% of the time, Pallas kernels for 0%

commit v1 on v0

v1 whole, which is shorter than its diff:
```python
import functools

import jax
import jax.numpy as jnp
from jax import lax
from jax.experimental import pallas as pl
from jax.experimental.pallas import tpu as pltpu
from jax.sharding import PartitionSpec as P

time_step = 0.125
epsilon = 1e-06
squarings = 5
taylor_terms = 12
MIB = 1 << 20
VMEM = pl.BlockSpec(memory_space=pltpu.VMEM)
SMEM = pl.BlockSpec(memory_space=pltpu.SMEM)
ANY = pl.BlockSpec(memory_space=pl.ANY)
LOAD_WIDTH = 256
LOAD_SLOTS = 6
PIECES = 4


def relative_order(devices):
    return list(range(0, devices, 2)) + list(range(1, devices, 2))


def load_kernel(devices, me_ref, a_ref, *refs):
    piece_refs, (slots, sems) = refs[:PIECES], refs[PIECES:]
    rows, extent = a_ref.shape
    width = slots.shape[2]
    block = extent // devices
    per_block = block // width
    steps = extent // width
    half = devices // 2
    me = me_ref[0]

    def source(step):
        place = step // per_block
        offset = jnp.where(place < half, 2 * place, 2 * (place - half) + 1)
        owner = jnp.bitwise_xor(me, offset)
        start = owner * block + (step % per_block) * width
        return a_ref.at[:, pl.ds(pl.multiple_of(start, width), width)]

    def copy(step):
        slot = step % LOAD_SLOTS
        return pltpu.make_async_copy(source(step), slots.at[slot], sems.at[slot])

    for step in range(min(LOAD_SLOTS, steps)):
        copy(step).start()

    per_piece = steps // PIECES
    for piece, piece_ref in enumerate(piece_refs):

        @pl.loop(0, per_piece)
        def _(inner):
            step = inner + piece * per_piece
            copy(step).wait()
            turned = slots[step % LOAD_SLOTS].T
            high = turned.astype(jnp.bfloat16)
            place = pl.ds(pl.multiple_of(inner * width, width), width)
            piece_ref[0, place, :] = high
            piece_ref[1, place, :] = (turned - high.astype(jnp.float32)).astype(jnp.bfloat16)

            @pl.when(step + LOAD_SLOTS < steps)
            def _():
                copy(step + LOAD_SLOTS).start()


def load_operator(local_coupling, me, devices):
    rows, extent = local_coupling.shape
    width = min(LOAD_WIDTH, extent // devices)

    return pl.pallas_call(
        functools.partial(load_kernel, devices),
        out_shape=(pltpu.VMEM((2, extent // PIECES, rows), jnp.bfloat16),) * PIECES,
        in_specs=[SMEM, ANY],
        out_specs=(VMEM,) * PIECES,
        scratch_shapes=[
            pltpu.VMEM((LOAD_SLOTS, rows, width), jnp.float32),
            pltpu.SemaphoreType.DMA((LOAD_SLOTS,)),
        ],
        compiler_params=pltpu.CompilerParams(vmem_limit_bytes=12 * MIB),
        cost_estimate=pl.CostEstimate(
            flops=1600 * rows * extent, bytes_accessed=4 * rows * extent, transcendentals=0
        ),
        name="load_operator",
    )(me, local_coupling)


def total(first, second):
    def each(block):
        return jnp.sum(jnp.sum(block, axis=0), axis=-1, keepdims=True)

    return each(first) + each(second)


def apply_rows(parts, piece_refs, split_ref, total_ref):
    count = 0
    for part in parts:
        for index in range(part.shape[0]):
            members = part.shape[1]
            block = part[index]
            high = block.astype(jnp.bfloat16)
            split_ref[count, :members] = high.astype(jnp.float32)
            split_ref[count, members:] = block - high.astype(jnp.float32)
            count += 1
    width = split_ref.shape[2]
    total_ref[...] = jnp.zeros_like(total_ref)

    per_piece = count // len(piece_refs)
    for piece, piece_ref in enumerate(piece_refs):

        @pl.loop(0, per_piece)
        def _(inner):
            lhs = split_ref[inner + piece * per_piece].astype(jnp.bfloat16)
            place = pl.ds(pl.multiple_of(inner * width, width), width)
            total_ref[...] += jnp.dot(
                lhs, piece_ref[0, place, :], preferred_element_type=jnp.float32
            ) + jnp.dot(lhs, piece_ref[1, place, :], preferred_element_type=jnp.float32)

    members = total_ref.shape[0] // 2
    return total_ref[:members] + total_ref[members:]


def first_kernel(xa_ref, xb_ref, damping_ref, *refs):
    piece_refs, (out_ref, split_ref, total_ref) = refs[:PIECES], refs[PIECES:]
    xa, xb = xa_ref[...], xb_ref[...]
    norm = jnp.sqrt(total(xa * xa, xb * xb) + epsilon)
    qa, qb = xa / norm[None], xb / norm[None]
    image = apply_rows([qa, qb], piece_refs, split_ref, total_ref)
    out_ref[...] = image - damping_ref[...] * qa[0]


def krylov(xa, xb, wa, wb):
    norm = jnp.sqrt(total(xa * xa, xb * xb) + epsilon)
    qa, qb = xa / norm[None], xb / norm[None]
    first = total(qa * wa, qb * wb)
    ra, rb = wa - first[None] * qa, wb - first[None] * qb
    length = jnp.sqrt(total(ra * ra, rb * rb) + epsilon)
    return norm, first, length, qa, ra / length[None], rb / length[None]


def second_kernel(
    xa_ref, xb_ref, wa_ref, wb_ref, damping_ref, *refs
):
    piece_refs, refs = refs[:PIECES], refs[PIECES:]
    partial_ref, scalars_ref, basis_ref, split_ref, total_ref = refs
    norm, first, length, qa, sa, sb = krylov(xa_ref[...], xb_ref[...], wa_ref[...], wb_ref[...])
    image = apply_rows([sa, sb], piece_refs, split_ref, total_ref)
    image = image - damping_ref[...] * sa[0]
    members = image.shape[0]
    for row, own in ((0, qa[0]), (1, sa[0])):
        inner = jnp.sum(own * image, axis=-1, keepdims=True)
        partial_ref[row] = jnp.broadcast_to(inner, (members, 128))
        basis_ref[row] = own
    for row, value in enumerate((norm, first, length)):
        scalars_ref[row] = jnp.broadcast_to(value, (members, 128))


def exponential(step_size, h00, h01, h10, h11):
    scale = 1.0 / 2.0**squarings
    s00, s01 = step_size * h00 * scale, step_size * h01 * scale
    s10, s11 = step_size * h10 * scale, step_size * h11 * scale
    one, zero = jnp.ones_like(h00), jnp.zeros_like(h00)
    r00, r01, r02, r10, r11, r12 = one, zero, zero, zero, one, zero
    for degree in range(taylor_terms, 0, -1):
        part = 1.0 / degree
        r00, r01, r02, r10, r11, r12 = (
            one + (s00 * r00 + s01 * r10) * part,
            (s00 * r01 + s01 * r11) * part,
            (s00 * r02 + s01 * r12 + scale) * part,
            (s10 * r00 + s11 * r10) * part,
            one + (s10 * r01 + s11 * r11) * part,
            (s10 * r02 + s11 * r12) * part,
        )
    for repeat in range(squarings):
        r00, r01, r02, r10, r11, r12 = (
            r00 * r00 + r01 * r10,
            r00 * r01 + r01 * r11,
            r00 * r02 + r01 * r12 + r02,
            r10 * r00 + r11 * r10,
            r10 * r01 + r11 * r11,
            r10 * r02 + r11 * r12 + r12,
        )
    return r00, r10, r02, r12


def combined(step_size, partial_refs, scalars_ref, basis_ref):
    inner = partial_refs[0][...]
    for ref in partial_refs[1:]:
        inner = inner + ref[...]
    norm, first, length = scalars_ref[0], scalars_ref[1], scalars_ref[2]
    e0, e1, f0, f1 = exponential(step_size, first, inner[0], length, inner[1])

    def spread(value):
        return value[:, :1]

    carried = basis_ref[0] * spread(norm * e0) + basis_ref[1] * spread(norm * e1)
    forced = basis_ref[0] * spread(step_size * norm * f0) + basis_ref[1] * spread(
        step_size * norm * f1
    )
    return carried, forced


def start_kernel(sums, members, counts_ref, *refs):
    partial_refs, (scalars_ref, basis_ref, state_ref, local_ref) = refs[:sums], refs[sums:]
    step_size = counts_ref[0].astype(jnp.float32) * time_step
    carried, forced = combined(step_size, partial_refs, scalars_ref, basis_ref)
    local_ref[...] = forced[members:]
    state_ref[...] = carried[:members] + forced[members:]


def next_kernel(sums, counts_ref, *refs):
    partial_refs, (scalars_ref, basis_ref, local_ref, state_ref) = refs[:sums], refs[sums:]
    step_size = counts_ref[0].astype(jnp.float32) * time_step
    carried, _ = combined(step_size, partial_refs, scalars_ref, basis_ref)
    state_ref[...] = carried + local_ref[...]


def permuted(array, tm_change, row_change):
    sections, devices = lax.axis_size("tm"), lax.axis_size("row")
    pairs = [
        (s * devices + r, (s ^ tm_change) * devices + (r ^ row_change))
        for s in range(sections)
        for r in range(devices)
    ]
    return lax.ppermute(array, ("tm", "row"), pairs)


def gathered(own, tm_change=0):
    devices = lax.axis_size("row")
    blocks = []
    for change in range(0, devices, 2):
        if change == 0 and tm_change == 0:
            blocks.append(own)
        else:
            blocks.append(permuted(own, tm_change, change))
    near = jnp.stack(blocks)
    return near, permuted(near, 0, 1)


def summed(partial):
    devices = lax.axis_size("row")
    pair = partial + permuted(partial, 0, 1)
    return [pair] + [permuted(pair, 0, change) for change in range(2, devices, 2)]


def on_device(coupling, damping, forcing, initial, counts):
    local_coupling = coupling[0]
    local_forcing = forcing[0]
    members, rows = initial.shape
    extent = local_coupling.shape[1]
    devices = lax.axis_size("row")
    sections = lax.axis_size("tm")
    slab_index = lax.axis_index("tm")
    me = lax.axis_index("row").astype(jnp.int32).reshape(1)

    operator = load_operator(local_coupling, me, devices)

    def scratch(batch):
        return [
            pltpu.VMEM((devices, 2 * batch, rows), jnp.float32),
            pltpu.VMEM((2 * batch, rows), jnp.float32),
        ]

    def cost(batch):
        return pl.CostEstimate(
            flops=16 * rows * extent, bytes_accessed=4 * rows * extent, transcendentals=0
        )

    params = pltpu.CompilerParams(vmem_limit_bytes=12 * MIB)

    def first_pass(xa, xb):
        batch = xa.shape[1]
        return pl.pallas_call(
            first_kernel,
            out_shape=jax.ShapeDtypeStruct((batch, rows), jnp.float32),
            in_specs=[VMEM] * (3 + PIECES),
            out_specs=VMEM,
            scratch_shapes=scratch(batch),
            compiler_params=params,
            cost_estimate=cost(batch),
            name="first_pass",
        )(xa, xb, damping, *operator)

    def second_pass(xa, xb, wa, wb):
        batch = xa.shape[1]
        return pl.pallas_call(
            second_kernel,
            out_shape=(
                jax.ShapeDtypeStruct((2, batch, 128), jnp.float32),
                jax.ShapeDtypeStruct((3, batch, 128), jnp.float32),
                jax.ShapeDtypeStruct((2, batch, rows), jnp.float32),
            ),
            in_specs=[VMEM] * (5 + PIECES),
            out_specs=(VMEM,) * 3,
            scratch_shapes=scratch(batch),
            compiler_params=params,
            cost_estimate=cost(batch),
            name="second_pass",
        )(xa, xb, wa, wb, damping, *operator)

    small = jax.ShapeDtypeStruct((members, rows), jnp.float32)
    xa, xb = gathered(jnp.concatenate([initial, local_forcing], axis=0))
    wa, wb = gathered(first_pass(xa, xb))
    partial, scalars, basis = second_pass(xa, xb, wa, wb)
    parts = summed(partial)
    state, local = pl.pallas_call(
        functools.partial(start_kernel, len(parts), members),
        out_shape=(small, small),
        in_specs=[SMEM] + [VMEM] * (len(parts) + 2),
        out_specs=(VMEM, VMEM),
        compiler_params=params,
        name="start_state",
    )(counts, *parts, scalars, basis)
    result = state
    for section in range(1, sections):
        xa, xb = gathered(state, (section - 1) ^ section)
        wa, wb = gathered(first_pass(xa, xb))
        partial, scalars, basis = second_pass(xa, xb, wa, wb)
        parts = summed(partial)
        state = pl.pallas_call(
            functools.partial(next_kernel, len(parts)),
            out_shape=small,
            in_specs=[SMEM] + [VMEM] * (len(parts) + 3),
            out_specs=VMEM,
            compiler_params=params,
            name="next_state",
        )(counts, *parts, scalars, basis, local)
        result = jnp.where(slab_index == section, state, result)
    return result[None]


def solution(mesh):
    placed = (P("tm", "row", None), P("tm", "row"), P("tm", None, "row"), P(None, "row"), P("tm"))
    return jax.shard_map(
        on_device, mesh=mesh, in_specs=placed, out_specs=P("tm", None, "row"), check_vma=False
    )
```

time: 628 us -> 191 us (0.30); the launches traced: 619 us -> 191 us
  matrix products: 383 us -> 0 us
  blocking collectives: 176 us -> 0 us
  Pallas kernels: 0 us -> 61.9 us
  starting transfers between devices: 12.2 us -> 63.3 us
  waiting for transfers between devices: 17.9 us -> 63.2 us
  other arithmetic: 16.1 us -> 1.53 us
  local copies, waits for them, and re-layouts: 11.7 us -> 0.01 us
    dot_general x115 -> x0, matrix products: 383 us -> none  [the longest x10 299 us: rows_product(): lax.dot_general(vectors, local_coupling, (((1,), (1,)), ((), ())), precis...]
    all_gather x12 -> x0, blocking collectives: 176 us -> none  [the longest x10 145 us: whole_arnoldi(): applied = lax.all_gather(applied_rows, 'row', axis=1, tiled=True)]
    pallas_call x0 -> x13, Pallas kernels: none -> 61.9 us  [the longest x4 24.6 us: second_pass(): pl.pallas_call(second_kernel, out_shape=(jax.ShapeDtypeStruct((2, batch,...]
    ppermute x3 -> x51, starting transfers between devices: 12.2 us -> 63.3 us  [permuted(): return lax.ppermute(array, ('tm', 'row'), pairs)]
    ppermute x3 -> x51, waiting for transfers between devices: 17.9 us -> 63.2 us  [permuted(): return lax.ppermute(array, ('tm', 'row'), pairs)]
    another operation x7 -> x9, other arithmetic: 10.2 us -> 0.88 us  [gathered(): near = jnp.stack(blocks)]
    scatter x25 -> x0, local copies, waits for them, and re-layouts: 6.71 us -> none  [the longest x5 6.42 us: exponent_block(): augmented = augmented.at[:, 0, KRYLOV].set(1.0)]
  transfers between devices with their start and end apart: 3 -> 51, of which waited for: 3 -> 35; matrix products, arithmetic and copies ran while one was open for 0% -> 0% of each run, Pallas kernels for 0% -> 7%
where the time goes in v1:
time: 191 us
  starting transfers between devices  63.3 us (33%)
  waiting for transfers between devices  63.2 us (33%)
  Pallas kernels  61.9 us (32%)
    ppermute x51, starting transfers between devices, permuted(): return lax.ppermute(array, ('tm', 'row'), pairs)  63.3 us
    ppermute x51, waiting for transfers between devices, permuted(): return lax.ppermute(array, ('tm', 'row'), pairs)  63.2 us
    pallas_call x4, Pallas kernels, second_pass(): pl.pallas_call(second_kernel, out_shape=(jax.ShapeDtypeStruct((2, batch,...  24.6 us
    pallas_call x4, Pallas kernels, first_pass(): pl.pallas_call(first_kernel, out_shape=jax.ShapeDtypeStruct((batch, rows)...  23.3 us
    pallas_call x1, Pallas kernels, load_operator(): pl.pallas_call(functools.partial(load_kernel, devices), out_shape=(pltpu....  13.4 us
  transfers between devices with their start and end apart: 51, of which 35 were waited for; matrix products, arithmetic and copies ran while one was open for 0% of the time, Pallas kernels for 7%

profile of v1, /device:TPU:0, one launch (start us, length us, event | category | flops | bytes accessed | tf_op | source)
XLA Modules:
  0.0 190.8 jit_solution(8155354571827232352)
XLA Ops:
  0.8 3.1 %collective-permute-start = (f32[16,1024]{1,0:T(8,128)S(1)}, f32[16,1024]{1,0:T(8,128)S(1)}, u32[]{:S(2)}, u32[]{:S(2)}) collective-permute-start(f32[16,1024]{1,0:T(8,128)S(1)} %get-tuple-element.42), channel_id=1, source_target_pairs={{0,2},{1,3},{2,0},{3,1},{4,6},{5,7},{6,4},{7,5},{8,10},{9,11},{10,... | collective-permute-start | bytes 196616 | tf_op jit(solution)/shard_map/ppermute | solution.py:227
  3.9 2.6 %collective-permute-start.1 = (f32[16,1024]{1,0:T(8,128)S(1)}, f32[16,1024]{1,0:T(8,128)S(1)}, u32[]{:S(2)}, u32[]{:S(2)}) collective-permute-start(f32[16,1024]{1,0:T(8,128)S(1)} %get-tuple-element.42), channel_id=1, source_target_pairs={{0,4},{1,5},{2,6},{3,7},{4,0},{5,1},{6,2},{7,3},{8,12},{9,13},{10,... | collective-permute-start | bytes 196616 | tf_op jit(solution)/shard_map/ppermute | solution.py:227
  6.5 4.7 %collective-permute-done.1 = f32[16,1024]{1,0:T(8,128)S(1)} collective-permute-done((f32[16,1024]{1,0:T(8,128)S(1)}, f32[16,1024]{1,0:T(8,128)S(1)}, u32[]{:S(2)}, u32[]{:S(2)}) %collective-permute-start.1) | collective-permute-done | bytes 65568 | tf_op jit(solution)/shard_map/ppermute | solution.py:227
  12.7 13.4 %load_operator.1 = (bf16[2,2048,1024]{2,1,0:T(8,128)(2,1)S(1)}, bf16[2,2048,1024]{2,1,0:T(8,128)(2,1)S(1)}, bf16[2,2048,1024]{2,1,0:T(8,128)(2,1)S(1)}, bf16[2,2048,1024]{2,1,0:T(8,128)(2,1)S(1)}) custom-call(s32[1]{0:T(128)} %bitcast.5.me_ref, f32[1024,8192]{1,0:T(8,128)} %bitcast.70), custom_call_target="tpu_custom_call" | custom-call | flops 13421772800 | bytes 33554432 | tf_op jit(solution)/shard_map/load_operator/pallas_call | solution.py:73
  26.1 6.9 %first_pass.4 = f32[16,1024]{1,0:T(8,128)S(1)} custom-call(f32[4,16,1024]{2,1,0:T(8,128)S(1)} %pad_maximum_fusion.xa_ref, f32[4,16,1024]{2,1,0:T(8,128)S(1)} %collective-permute-done.3.xb_ref, f32[1,1024]{1,0:T(1,128)S(1)} %copy-done, bf16[2,2048,1024]{2,1,0:T(8,128)(2,1)S(1)} %get-tuple-element.23.refs_0_, ...), custom_call_target="tpu_custom_call" | custom-call | flops 134217728 | bytes 33554432 | tf_op jit(solution)/shard_map/first_pass/pallas_call | solution.py:275
  33.0 1.8 collective-permute-start.6
  35.2 2.3 %collective-permute-start.5 = (f32[16,1024]{1,0:T(8,128)S(1)}, f32[16,1024]{1,0:T(8,128)S(1)}, u32[]{:S(2)}, u32[]{:S(2)}) collective-permute-start(f32[16,1024]{1,0:T(8,128)S(1)} %first_pass.4), channel_id=1, source_target_pairs={{0,4},{1,5},{2,6},{3,7},{4,0},{5,1},{6,2},{7,3},{8,12},{9,13},{10,... | collective-permute-start | bytes 196616 | tf_op jit(solution)/shard_map/ppermute | solution.py:227
  37.4 2.4 %collective-permute-done.6 = f32[16,1024]{1,0:T(8,128)S(1)} collective-permute-done((f32[16,1024]{1,0:T(8,128)S(1)}, f32[16,1024]{1,0:T(8,128)S(1)}, u32[]{:S(2)}, u32[]{:S(2)}) %collective-permute-start.6) | collective-permute-done | bytes 65568 | tf_op jit(solution)/shard_map/ppermute | solution.py:227
  39.8 2.0 %collective-permute-done.4 = f32[16,1024]{1,0:T(8,128)S(1)} collective-permute-done((f32[16,1024]{1,0:T(8,128)S(1)}, f32[16,1024]{1,0:T(8,128)S(1)}, u32[]{:S(2)}, u32[]{:S(2)}) %collective-permute-start.4) | collective-permute-done | bytes 65568 | tf_op jit(solution)/shard_map/ppermute | solution.py:227
  41.9 1.5 collective-permute-done.7.wb_ref
  43.4 7.3 %second_pass.4 = (f32[2,16,128]{2,1,0:T(8,128)S(1)}, f32[3,16,128]{2,1,0:T(8,128)S(1)}, f32[2,16,1024]{2,1,0:T(8,128)S(1)}) custom-call(f32[4,16,1024]{2,1,0:T(8,128)S(1)} %pad_maximum_fusion.xa_ref, f32[4,16,1024]{2,1,0:T(8,128)S(1)} %collective-permute-done.3.xb_ref, f32[4,16,1024]{2,1,0:T(8,128)S(1)} %pad_maximum_fusion.1.wa_ref, ...), custom_call_target="tpu_custom_call" | custom-call | flops 134217728 | bytes 33554432 | tf_op jit(solution)/shard_map/second_pass/pallas_call | solution.py:288
  53.2 2.0 %collective-permute-start.11 = (f32[2,16,128]{2,1,0:T(8,128)S(1)}, f32[2,16,128]{2,1,0:T(8,128)S(1)}, u32[]{:S(2)}, u32[]{:S(2)}) collective-permute-start(f32[2,16,128]{2,1,0:T(8,128)S(1)} %add.12.refs_0_), channel_id=1, source_target_pairs={{0,6},{1,7},{2,4},{3,5},{4,2},{5,3},{6,0},{7,1},{8,14},{9,15},{10,... | collective-permute-start | bytes 49160 | tf_op jit(solution)/shard_map/ppermute | solution.py:227
  56.6 2.2 %collective-permute-done.11.refs_3_ = f32[2,16,128]{2,1,0:T(8,128)S(1)} collective-permute-done((f32[2,16,128]{2,1,0:T(8,128)S(1)}, f32[2,16,128]{2,1,0:T(8,128)S(1)}, u32[]{:S(2)}, u32[]{:S(2)}) %collective-permute-start.11) | collective-permute-done | bytes 16416 | tf_op jit(solution)/shard_map/ppermute | solution.py:227
  59.1 1.5 collective-permute-start.12
  60.9 3.2 %collective-permute-start.14 = (f32[8,1024]{1,0:T(8,128)S(1)}, f32[8,1024]{1,0:T(8,128)S(1)}, u32[]{:S(2)}, u32[]{:S(2)}) collective-permute-start(f32[8,1024]{1,0:T(8,128)S(1)} %get-tuple-element.30), channel_id=1, source_target_pairs={{0,12},{1,13},{2,14},{3,15},{4,8},{5,9},{6,10},{7,11},{8,4},{9,5},... | collective-permute-start | bytes 98312 | tf_op jit(solution)/shard_map/ppermute | solution.py:227
  64.1 1.8 collective-permute-start.15
  66.6 4.1 %collective-permute-done.15 = f32[8,1024]{1,0:T(8,128)S(1)} collective-permute-done((f32[8,1024]{1,0:T(8,128)S(1)}, f32[8,1024]{1,0:T(8,128)S(1)}, u32[]{:S(2)}, u32[]{:S(2)}) %collective-permute-start.15) | collective-permute-done | bytes 32800 | tf_op jit(solution)/shard_map/ppermute | solution.py:227
  72.2 5.5 %first_pass.5 = f32[8,1024]{1,0:T(8,128)S(1)} custom-call(f32[4,8,1024]{2,1,0:T(8,128)S(1)} %pad_maximum_fusion.2.xa_ref, f32[4,8,1024]{2,1,0:T(8,128)S(1)} %collective-permute-done.16.xb_ref, f32[1,1024]{1,0:T(1,128)S(1)} %copy-done, bf16[2,2048,1024]{2,1,0:T(8,128)(2,1)S(1)} %get-tuple-element.23.refs_0_, ...), custom_call_target="tpu_custom_call" | custom-call | flops 134217728 | bytes 33554432 | tf_op jit(solution)/shard_map/first_pass/pallas_call | solution.py:275
  77.6 2.4 %collective-permute-start.18 = (f32[8,1024]{1,0:T(8,128)S(1)}, f32[8,1024]{1,0:T(8,128)S(1)}, u32[]{:S(2)}, u32[]{:S(2)}) collective-permute-start(f32[8,1024]{1,0:T(8,128)S(1)} %first_pass.5), channel_id=1, source_target_pairs={{0,4},{1,5},{2,6},{3,7},{4,0},{5,1},{6,2},{7,3},{8,12},{9,13},{10,... | collective-permute-start | bytes 98312 | tf_op jit(solution)/shard_map/ppermute | solution.py:227
  80.0 2.0 %collective-permute-start.19 = (f32[8,1024]{1,0:T(8,128)S(1)}, f32[8,1024]{1,0:T(8,128)S(1)}, u32[]{:S(2)}, u32[]{:S(2)}) collective-permute-start(f32[8,1024]{1,0:T(8,128)S(1)} %first_pass.5), channel_id=1, source_target_pairs={{0,6},{1,7},{2,4},{3,5},{4,2},{5,3},{6,0},{7,1},{8,14},{9,15},{10,... | collective-permute-start | bytes 98312 | tf_op jit(solution)/shard_map/ppermute | solution.py:227
  83.1 2.7 %collective-permute-done.19 = f32[8,1024]{1,0:T(8,128)S(1)} collective-permute-done((f32[8,1024]{1,0:T(8,128)S(1)}, f32[8,1024]{1,0:T(8,128)S(1)}, u32[]{:S(2)}, u32[]{:S(2)}) %collective-permute-start.19) | collective-permute-done | bytes 32800 | tf_op jit(solution)/shard_map/ppermute | solution.py:227
  87.2 5.8 %second_pass.5 = (f32[2,8,128]{2,1,0:T(8,128)S(1)}, f32[3,8,128]{2,1,0:T(8,128)S(1)}, f32[2,8,1024]{2,1,0:T(8,128)S(1)}) custom-call(f32[4,8,1024]{2,1,0:T(8,128)S(1)} %pad_maximum_fusion.2.xa_ref, f32[4,8,1024]{2,1,0:T(8,128)S(1)} %collective-permute-done.16.xb_ref, f32[4,8,1024]{2,1,0:T(8,128)S(1)} %pad_maximum_fusion.3.wa_ref, ...), custom_call_target="tpu_custom_call" | custom-call | flops 134217728 | bytes 33554432 | tf_op jit(solution)/shard_map/second_pass/pallas_call | solution.py:288
  94.1 2.5 %collective-permute-start.23 = (f32[2,8,128]{2,1,0:T(8,128)S(1)}, f32[2,8,128]{2,1,0:T(8,128)S(1)}, u32[]{:S(2)}, u32[]{:S(2)}) collective-permute-start(f32[2,8,128]{2,1,0:T(8,128)S(1)} %add.13.refs_0_), channel_id=1, source_target_pairs={{0,4},{1,5},{2,6},{3,7},{4,0},{5,1},{6,2},{7,3},{8,12},{9,13},{10,... | collective-permute-start | bytes 24584 | tf_op jit(solution)/shard_map/ppermute | solution.py:227
  96.7 1.9 collective-permute-start.24
  98.8 3.4 %collective-permute-done.24.refs_3_ = f32[2,8,128]{2,1,0:T(8,128)S(1)} collective-permute-done((f32[2,8,128]{2,1,0:T(8,128)S(1)}, f32[2,8,128]{2,1,0:T(8,128)S(1)}, u32[]{:S(2)}, u32[]{:S(2)}) %collective-permute-start.24) | collective-permute-done | bytes 8224 | tf_op jit(solution)/shard_map/ppermute | solution.py:227
  102.3 1.5 collective-permute-start.25
  103.8 4.2 %collective-permute-start.27 = (f32[8,1024]{1,0:T(8,128)S(1)}, f32[8,1024]{1,0:T(8,128)S(1)}, u32[]{:S(2)}, u32[]{:S(2)}) collective-permute-start(f32[8,1024]{1,0:T(8,128)S(1)} %next_state.3), channel_id=1, source_target_pairs={{0,28},{1,29},{2,30},{3,31},{4,24},{5,25},{6,26},{7,27},{8,20},{9,... | collective-permute-start | bytes 98312 | tf_op jit(solution)/shard_map/ppermute | solution.py:227
  108.0 2.8 %collective-permute-start.28 = (f32[8,1024]{1,0:T(8,128)S(1)}, f32[8,1024]{1,0:T(8,128)S(1)}, u32[]{:S(2)}, u32[]{:S(2)}) collective-permute-start(f32[8,1024]{1,0:T(8,128)S(1)} %next_state.3), channel_id=1, source_target_pairs={{0,30},{1,31},{2,28},{3,29},{4,26},{5,27},{6,24},{7,25},{8,22},{9,... | collective-permute-start | bytes 98312 | tf_op jit(solution)/shard_map/ppermute | solution.py:227
  110.8 4.7 %collective-permute-done.28 = f32[8,1024]{1,0:T(8,128)S(1)} collective-permute-done((f32[8,1024]{1,0:T(8,128)S(1)}, f32[8,1024]{1,0:T(8,128)S(1)}, u32[]{:S(2)}, u32[]{:S(2)}) %collective-permute-start.28) | collective-permute-done | bytes 32800 | tf_op jit(solution)/shard_map/ppermute | solution.py:227
  116.9 5.5 %first_pass.6 = f32[8,1024]{1,0:T(8,128)S(1)} custom-call(f32[4,8,1024]{2,1,0:T(8,128)S(1)} %pad_maximum_fusion.4.xa_ref, f32[4,8,1024]{2,1,0:T(8,128)S(1)} %collective-permute-done.29.xb_ref, f32[1,1024]{1,0:T(1,128)S(1)} %copy-done, bf16[2,2048,1024]{2,1,0:T(8,128)(2,1)S(1)} %get-tuple-element.23.refs_0_, ...), custom_call_target="tpu_custom_call" | custom-call | flops 134217728 | bytes 33554432 | tf_op jit(solution)/shard_map/first_pass/pallas_call | solution.py:275
  122.5 2.5 %collective-permute-start.31 = (f32[8,1024]{1,0:T(8,128)S(1)}, f32[8,1024]{1,0:T(8,128)S(1)}, u32[]{:S(2)}, u32[]{:S(2)}) collective-permute-start(f32[8,1024]{1,0:T(8,128)S(1)} %first_pass.6), channel_id=1, source_target_pairs={{0,4},{1,5},{2,6},{3,7},{4,0},{5,1},{6,2},{7,3},{8,12},{9,13},{10,... | collective-permute-start | bytes 98312 | tf_op jit(solution)/shard_map/ppermute | solution.py:227
  125.0 1.9 collective-permute-start.32
  128.0 2.7 %collective-permute-done.32 = f32[8,1024]{1,0:T(8,128)S(1)} collective-permute-done((f32[8,1024]{1,0:T(8,128)S(1)}, f32[8,1024]{1,0:T(8,128)S(1)}, u32[]{:S(2)}, u32[]{:S(2)}) %collective-permute-start.32) | collective-permute-done | bytes 32800 | tf_op jit(solution)/shard_map/ppermute | solution.py:227
  132.1 5.8 %second_pass.6 = (f32[2,8,128]{2,1,0:T(8,128)S(1)}, f32[3,8,128]{2,1,0:T(8,128)S(1)}, f32[2,8,1024]{2,1,0:T(8,128)S(1)}) custom-call(f32[4,8,1024]{2,1,0:T(8,128)S(1)} %pad_maximum_fusion.4.xa_ref, f32[4,8,1024]{2,1,0:T(8,128)S(1)} %collective-permute-done.29.xb_ref, f32[4,8,1024]{2,1,0:T(8,128)S(1)} %pad_maximum_fusion.5.wa_ref, ...), custom_call_target="tpu_custom_call" | custom-call | flops 134217728 | bytes 33554432 | tf_op jit(solution)/shard_map/second_pass/pallas_call | solution.py:288
  139.1 2.4 %collective-permute-start.36 = (f32[2,8,128]{2,1,0:T(8,128)S(1)}, f32[2,8,128]{2,1,0:T(8,128)S(1)}, u32[]{:S(2)}, u32[]{:S(2)}) collective-permute-start(f32[2,8,128]{2,1,0:T(8,128)S(1)} %add.14.refs_0_), channel_id=1, source_target_pairs={{0,4},{1,5},{2,6},{3,7},{4,0},{5,1},{6,2},{7,3},{8,12},{9,13},{10,... | collective-permute-start | bytes 24584 | tf_op jit(solution)/shard_map/ppermute | solution.py:227
  141.5 2.0 %collective-permute-start.37 = (f32[2,8,128]{2,1,0:T(8,128)S(1)}, f32[2,8,128]{2,1,0:T(8,128)S(1)}, u32[]{:S(2)}, u32[]{:S(2)}) collective-permute-start(f32[2,8,128]{2,1,0:T(8,128)S(1)} %add.14.refs_0_), channel_id=1, source_target_pairs={{0,6},{1,7},{2,4},{3,5},{4,2},{5,3},{6,0},{7,1},{8,14},{9,15},{10,... | collective-permute-start | bytes 24584 | tf_op jit(solution)/shard_map/ppermute | solution.py:227
  143.6 3.3 %collective-permute-done.37.refs_3_ = f32[2,8,128]{2,1,0:T(8,128)S(1)} collective-permute-done((f32[2,8,128]{2,1,0:T(8,128)S(1)}, f32[2,8,128]{2,1,0:T(8,128)S(1)}, u32[]{:S(2)}, u32[]{:S(2)}) %collective-permute-start.37) | collective-permute-done | bytes 8224 | tf_op jit(solution)/shard_map/ppermute | solution.py:227
  148.6 3.4 %collective-permute-start.40 = (f32[8,1024]{1,0:T(8,128)S(1)}, f32[8,1024]{1,0:T(8,128)S(1)}, u32[]{:S(2)}, u32[]{:S(2)}) collective-permute-start(f32[8,1024]{1,0:T(8,128)S(1)} %next_state.4), channel_id=1, source_target_pairs={{0,12},{1,13},{2,14},{3,15},{4,8},{5,9},{6,10},{7,11},{8,4},{9,5},... | collective-permute-start | bytes 98312 | tf_op jit(solution)/shard_map/ppermute | solution.py:227
  152.0 1.8 collective-permute-start.41
  154.3 4.3 %collective-permute-done.41 = f32[8,1024]{1,0:T(8,128)S(1)} collective-permute-done((f32[8,1024]{1,0:T(8,128)S(1)}, f32[8,1024]{1,0:T(8,128)S(1)}, u32[]{:S(2)}, u32[]{:S(2)}) %collective-permute-start.41) | collective-permute-done | bytes 32800 | tf_op jit(solution)/shard_map/ppermute | solution.py:227
  160.1 5.5 %first_pass.7 = f32[8,1024]{1,0:T(8,128)S(1)} custom-call(f32[4,8,1024]{2,1,0:T(8,128)S(1)} %pad_maximum_fusion.6.xa_ref, f32[4,8,1024]{2,1,0:T(8,128)S(1)} %collective-permute-done.42.xb_ref, f32[1,1024]{1,0:T(1,128)S(1)} %copy-done, bf16[2,2048,1024]{2,1,0:T(8,128)(2,1)S(1)} %get-tuple-element.23.refs_0_, ...), custom_call_target="tpu_custom_call" | custom-call | flops 134217728 | bytes 33554432 | tf_op jit(solution)/shard_map/first_pass/pallas_call | solution.py:275
  165.6 2.4 %collective-permute-start.44 = (f32[8,1024]{1,0:T(8,128)S(1)}, f32[8,1024]{1,0:T(8,128)S(1)}, u32[]{:S(2)}, u32[]{:S(2)}) collective-permute-start(f32[8,1024]{1,0:T(8,128)S(1)} %first_pass.7), channel_id=1, source_target_pairs={{0,4},{1,5},{2,6},{3,7},{4,0},{5,1},{6,2},{7,3},{8,12},{9,13},{10,... | collective-permute-start | bytes 98312 | tf_op jit(solution)/shard_map/ppermute | solution.py:227
  168.0 2.0 %collective-permute-start.45 = (f32[8,1024]{1,0:T(8,128)S(1)}, f32[8,1024]{1,0:T(8,128)S(1)}, u32[]{:S(2)}, u32[]{:S(2)}) collective-permute-start(f32[8,1024]{1,0:T(8,128)S(1)} %first_pass.7), channel_id=1, source_target_pairs={{0,6},{1,7},{2,4},{3,5},{4,2},{5,3},{6,0},{7,1},{8,14},{9,15},{10,... | collective-permute-start | bytes 98312 | tf_op jit(solution)/shard_map/ppermute | solution.py:227
  171.0 2.7 %collective-permute-done.45 = f32[8,1024]{1,0:T(8,128)S(1)} collective-permute-done((f32[8,1024]{1,0:T(8,128)S(1)}, f32[8,1024]{1,0:T(8,128)S(1)}, u32[]{:S(2)}, u32[]{:S(2)}) %collective-permute-start.45) | collective-permute-done | bytes 32800 | tf_op jit(solution)/shard_map/ppermute | solution.py:227
  175.1 5.8 %second_pass.7 = (f32[2,8,128]{2,1,0:T(8,128)S(1)}, f32[3,8,128]{2,1,0:T(8,128)S(1)}, f32[2,8,1024]{2,1,0:T(8,128)S(1)}) custom-call(f32[4,8,1024]{2,1,0:T(8,128)S(1)} %pad_maximum_fusion.6.xa_ref, f32[4,8,1024]{2,1,0:T(8,128)S(1)} %collective-permute-done.42.xb_ref, f32[4,8,1024]{2,1,0:T(8,128)S(1)} %pad_maximum_fusion.7.wa_ref, ...), custom_call_target="tpu_custom_call" | custom-call | flops 134217728 | bytes 33554432 | tf_op jit(solution)/shard_map/second_pass/pallas_call | solution.py:288
  182.1 2.5 %collective-permute-start.49 = (f32[2,8,128]{2,1,0:T(8,128)S(1)}, f32[2,8,128]{2,1,0:T(8,128)S(1)}, u32[]{:S(2)}, u32[]{:S(2)}) collective-permute-start(f32[2,8,128]{2,1,0:T(8,128)S(1)} %add.15.refs_0_), channel_id=1, source_target_pairs={{0,4},{1,5},{2,6},{3,7},{4,0},{5,1},{6,2},{7,3},{8,12},{9,13},{10,... | collective-permute-start | bytes 24584 | tf_op jit(solution)/shard_map/ppermute | solution.py:227
  184.6 1.9 collective-permute-start.50
  186.7 3.4 %collective-permute-done.50.refs_3_ = f32[2,8,128]{2,1,0:T(8,128)S(1)} collective-permute-done((f32[2,8,128]{2,1,0:T(8,128)S(1)}, f32[2,8,128]{2,1,0:T(8,128)S(1)}, u32[]{:S(2)}, u32[]{:S(2)}) %collective-permute-start.50) | collective-permute-done | bytes 8224 | tf_op jit(solution)/shard_map/ppermute | solution.py:227
  (83 shorter events, 26.2 us)
Async XLA Ops:
  0.8 5.7 %collective-permute-start = (f32[16,1024]{1,0:T(8,128)S(1)}, f32[16,1024]{1,0:T(8,128)S(1)}, u32[]{:S(2)}, u32[]{:S(2)}) collective-permute-start(f32[16,1024]{1,0:T(8,128)S(1)} %get-tuple-element.42), channel_id=1, source_target_pairs={{0,2},{1,3},{2,0},{3,1},{4,6},{5,7},{6,4},{7,5},{8,10},{9,11},{10,... | collective-permute-start | bytes 196616 | tf_op jit(solution)/shard_map/ppermute | solution.py:227
  3.9 7.3 %collective-permute-start.1 = (f32[16,1024]{1,0:T(8,128)S(1)}, f32[16,1024]{1,0:T(8,128)S(1)}, u32[]{:S(2)}, u32[]{:S(2)}) collective-permute-start(f32[16,1024]{1,0:T(8,128)S(1)} %get-tuple-element.42), channel_id=1, source_target_pairs={{0,4},{1,5},{2,6},{3,7},{4,0},{5,1},{6,2},{7,3},{8,12},{9,13},{10,... | collective-permute-start | bytes 196616 | tf_op jit(solution)/shard_map/ppermute | solution.py:227
  6.5 6.1 %collective-permute-start.2 = (f32[16,1024]{1,0:T(8,128)S(1)}, f32[16,1024]{1,0:T(8,128)S(1)}, u32[]{:S(2)}, u32[]{:S(2)}) collective-permute-start(f32[16,1024]{1,0:T(8,128)S(1)} %get-tuple-element.42), channel_id=1, source_target_pairs={{0,6},{1,7},{2,4},{3,5},{4,2},{5,3},{6,0},{7,1},{8,14},{9,15},{10,... | collective-permute-start | bytes 196616 | tf_op jit(solution)/shard_map/ppermute | solution.py:227
  12.6 13.5 %collective-permute-start.3 = (f32[4,16,1024]{2,1,0:T(8,128)S(1)}, f32[4,16,1024]{2,1,0:T(8,128)S(1)}, u32[]{:S(2)}, u32[]{:S(2)}) collective-permute-start(f32[4,16,1024]{2,1,0:T(8,128)S(1)} %pad_maximum_fusion.xa_ref), channel_id=1, source_target_pairs={{0,1},{1,0},{2,3},{3,2},{4,5},{5,4},{6,7},{7,6},{8,9},{9,8},{10,11... | collective-permute-start | bytes 786440 | tf_op jit(solution)/shard_map/ppermute | solution.py:227
  33.0 6.9 %collective-permute-start.6 = (f32[16,1024]{1,0:T(8,128)S(1)}, f32[16,1024]{1,0:T(8,128)S(1)}, u32[]{:S(2)}, u32[]{:S(2)}) collective-permute-start(f32[16,1024]{1,0:T(8,128)S(1)} %first_pass.4), channel_id=1, source_target_pairs={{0,6},{1,7},{2,4},{3,5},{4,2},{5,3},{6,0},{7,1},{8,14},{9,15},{10,... | collective-permute-start | bytes 196616 | tf_op jit(solution)/shard_map/ppermute | solution.py:227
  34.8 7.0 %collective-permute-start.4 = (f32[16,1024]{1,0:T(8,128)S(1)}, f32[16,1024]{1,0:T(8,128)S(1)}, u32[]{:S(2)}, u32[]{:S(2)}) collective-permute-start(f32[16,1024]{1,0:T(8,128)S(1)} %first_pass.4), channel_id=1, source_target_pairs={{0,2},{1,3},{2,0},{3,1},{4,6},{5,7},{6,4},{7,5},{8,10},{9,11},{10,... | collective-permute-start | bytes 196616 | tf_op jit(solution)/shard_map/ppermute | solution.py:227
  35.2 6.7 %collective-permute-start.5 = (f32[16,1024]{1,0:T(8,128)S(1)}, f32[16,1024]{1,0:T(8,128)S(1)}, u32[]{:S(2)}, u32[]{:S(2)}) collective-permute-start(f32[16,1024]{1,0:T(8,128)S(1)} %first_pass.4), channel_id=1, source_target_pairs={{0,4},{1,5},{2,6},{3,7},{4,0},{5,1},{6,2},{7,3},{8,12},{9,13},{10,... | collective-permute-start | bytes 196616 | tf_op jit(solution)/shard_map/ppermute | solution.py:227
  41.8 1.6 collective-permute-start.7
  50.8 1.2 collective-permute-start.8
  51.9 4.6 %collective-permute-start.10 = (f32[2,16,128]{2,1,0:T(8,128)S(1)}, f32[2,16,128]{2,1,0:T(8,128)S(1)}, u32[]{:S(2)}, u32[]{:S(2)}) collective-permute-start(f32[2,16,128]{2,1,0:T(8,128)S(1)} %add.12.refs_0_), channel_id=1, source_target_pairs={{0,4},{1,5},{2,6},{3,7},{4,0},{5,1},{6,2},{7,3},{8,12},{9,13},{10,... | collective-permute-start | bytes 49160 | tf_op jit(solution)/shard_map/ppermute | solution.py:227
  53.2 5.5 %collective-permute-start.11 = (f32[2,16,128]{2,1,0:T(8,128)S(1)}, f32[2,16,128]{2,1,0:T(8,128)S(1)}, u32[]{:S(2)}, u32[]{:S(2)}) collective-permute-start(f32[2,16,128]{2,1,0:T(8,128)S(1)} %add.12.refs_0_), channel_id=1, source_target_pairs={{0,6},{1,7},{2,4},{3,5},{4,2},{5,3},{6,0},{7,1},{8,14},{9,15},{10,... | collective-permute-start | bytes 49160 | tf_op jit(solution)/shard_map/ppermute | solution.py:227
  55.2 3.7 %collective-permute-start.9 = (f32[2,16,128]{2,1,0:T(8,128)S(1)}, f32[2,16,128]{2,1,0:T(8,128)S(1)}, u32[]{:S(2)}, u32[]{:S(2)}) collective-permute-start(f32[2,16,128]{2,1,0:T(8,128)S(1)} %add.12.refs_0_), channel_id=1, source_target_pairs={{0,2},{1,3},{2,0},{3,1},{4,6},{5,7},{6,4},{7,5},{8,10},{9,11},{10,... | collective-permute-start | bytes 49160 | tf_op jit(solution)/shard_map/ppermute | solution.py:227
  59.1 6.8 %collective-permute-start.12 = (f32[8,1024]{1,0:T(8,128)S(1)}, f32[8,1024]{1,0:T(8,128)S(1)}, u32[]{:S(2)}, u32[]{:S(2)}) collective-permute-start(f32[8,1024]{1,0:T(8,128)S(1)} %get-tuple-element.30), channel_id=1, source_target_pairs={{0,8},{1,9},{2,10},{3,11},{4,12},{5,13},{6,14},{7,15},{8,0},{9,1},... | collective-permute-start | bytes 98312 | tf_op jit(solution)/shard_map/ppermute | solution.py:227
  60.7 5.3 %collective-permute-start.13 = (f32[8,1024]{1,0:T(8,128)S(1)}, f32[8,1024]{1,0:T(8,128)S(1)}, u32[]{:S(2)}, u32[]{:S(2)}) collective-permute-start(f32[8,1024]{1,0:T(8,128)S(1)} %get-tuple-element.30), channel_id=1, source_target_pairs={{0,10},{1,11},{2,8},{3,9},{4,14},{5,15},{6,12},{7,13},{8,2},{9,3},... | collective-permute-start | bytes 98312 | tf_op jit(solution)/shard_map/ppermute | solution.py:227
  60.9 5.7 %collective-permute-start.14 = (f32[8,1024]{1,0:T(8,128)S(1)}, f32[8,1024]{1,0:T(8,128)S(1)}, u32[]{:S(2)}, u32[]{:S(2)}) collective-permute-start(f32[8,1024]{1,0:T(8,128)S(1)} %get-tuple-element.30), channel_id=1, source_target_pairs={{0,12},{1,13},{2,14},{3,15},{4,8},{5,9},{6,10},{7,11},{8,4},{9,5},... | collective-permute-start | bytes 98312 | tf_op jit(solution)/shard_map/ppermute | solution.py:227
  64.1 6.6 %collective-permute-start.15 = (f32[8,1024]{1,0:T(8,128)S(1)}, f32[8,1024]{1,0:T(8,128)S(1)}, u32[]{:S(2)}, u32[]{:S(2)}) collective-permute-start(f32[8,1024]{1,0:T(8,128)S(1)} %get-tuple-element.30), channel_id=1, source_target_pairs={{0,14},{1,15},{2,12},{3,13},{4,10},{5,11},{6,8},{7,9},{8,6},{9,7},... | collective-permute-start | bytes 98312 | tf_op jit(solution)/shard_map/ppermute | solution.py:227
  70.7 1.4 collective-permute-start.16
  77.6 4.4 %collective-permute-start.17 = (f32[8,1024]{1,0:T(8,128)S(1)}, f32[8,1024]{1,0:T(8,128)S(1)}, u32[]{:S(2)}, u32[]{:S(2)}) collective-permute-start(f32[8,1024]{1,0:T(8,128)S(1)} %first_pass.5), channel_id=1, source_target_pairs={{0,2},{1,3},{2,0},{3,1},{4,6},{5,7},{6,4},{7,5},{8,10},{9,11},{10,... | collective-permute-start | bytes 98312 | tf_op jit(solution)/shard_map/ppermute | solution.py:227
  77.6 5.4 %collective-permute-start.18 = (f32[8,1024]{1,0:T(8,128)S(1)}, f32[8,1024]{1,0:T(8,128)S(1)}, u32[]{:S(2)}, u32[]{:S(2)}) collective-permute-start(f32[8,1024]{1,0:T(8,128)S(1)} %first_pass.5), channel_id=1, source_target_pairs={{0,4},{1,5},{2,6},{3,7},{4,0},{5,1},{6,2},{7,3},{8,12},{9,13},{10,... | collective-permute-start | bytes 98312 | tf_op jit(solution)/shard_map/ppermute | solution.py:227
  80.0 5.7 %collective-permute-start.19 = (f32[8,1024]{1,0:T(8,128)S(1)}, f32[8,1024]{1,0:T(8,128)S(1)}, u32[]{:S(2)}, u32[]{:S(2)}) collective-permute-start(f32[8,1024]{1,0:T(8,128)S(1)} %first_pass.5), channel_id=1, source_target_pairs={{0,6},{1,7},{2,4},{3,5},{4,2},{5,3},{6,0},{7,1},{8,14},{9,15},{10,... | collective-permute-start | bytes 98312 | tf_op jit(solution)/shard_map/ppermute | solution.py:227
  85.8 1.4 collective-permute-start.20
  94.1 4.4 %collective-permute-start.22 = (f32[2,8,128]{2,1,0:T(8,128)S(1)}, f32[2,8,128]{2,1,0:T(8,128)S(1)}, u32[]{:S(2)}, u32[]{:S(2)}) collective-permute-start(f32[2,8,128]{2,1,0:T(8,128)S(1)} %add.13.refs_0_), channel_id=1, source_target_pairs={{0,2},{1,3},{2,0},{3,1},{4,6},{5,7},{6,4},{7,5},{8,10},{9,11},{10,... | collective-permute-start | bytes 24584 | tf_op jit(solution)/shard_map/ppermute | solution.py:227
  94.1 4.6 %collective-permute-start.23 = (f32[2,8,128]{2,1,0:T(8,128)S(1)}, f32[2,8,128]{2,1,0:T(8,128)S(1)}, u32[]{:S(2)}, u32[]{:S(2)}) collective-permute-start(f32[2,8,128]{2,1,0:T(8,128)S(1)} %add.13.refs_0_), channel_id=1, source_target_pairs={{0,4},{1,5},{2,6},{3,7},{4,0},{5,1},{6,2},{7,3},{8,12},{9,13},{10,... | collective-permute-start | bytes 24584 | tf_op jit(solution)/shard_map/ppermute | solution.py:227
  96.7 5.4 %collective-permute-start.24 = (f32[2,8,128]{2,1,0:T(8,128)S(1)}, f32[2,8,128]{2,1,0:T(8,128)S(1)}, u32[]{:S(2)}, u32[]{:S(2)}) collective-permute-start(f32[2,8,128]{2,1,0:T(8,128)S(1)} %add.13.refs_0_), channel_id=1, source_target_pairs={{0,6},{1,7},{2,4},{3,5},{4,2},{5,3},{6,0},{7,1},{8,14},{9,15},{10,... | collective-permute-start | bytes 24584 | tf_op jit(solution)/shard_map/ppermute | solution.py:227
  102.3 8.6 %collective-permute-start.25 = (f32[8,1024]{1,0:T(8,128)S(1)}, f32[8,1024]{1,0:T(8,128)S(1)}, u32[]{:S(2)}, u32[]{:S(2)}) collective-permute-start(f32[8,1024]{1,0:T(8,128)S(1)} %next_state.3), channel_id=1, source_target_pairs={{0,24},{1,25},{2,26},{3,27},{4,28},{5,29},{6,30},{7,31},{8,16},{9,... | collective-permute-start | bytes 98312 | tf_op jit(solution)/shard_map/ppermute | solution.py:227
  103.8 7.1 %collective-permute-start.26 = (f32[8,1024]{1,0:T(8,128)S(1)}, f32[8,1024]{1,0:T(8,128)S(1)}, u32[]{:S(2)}, u32[]{:S(2)}) collective-permute-start(f32[8,1024]{1,0:T(8,128)S(1)} %next_state.3), channel_id=1, source_target_pairs={{0,26},{1,27},{2,24},{3,25},{4,30},{5,31},{6,28},{7,29},{8,18},{9,... | collective-permute-start | bytes 98312 | tf_op jit(solution)/shard_map/ppermute | solution.py:227
  103.8 7.1 %collective-permute-start.27 = (f32[8,1024]{1,0:T(8,128)S(1)}, f32[8,1024]{1,0:T(8,128)S(1)}, u32[]{:S(2)}, u32[]{:S(2)}) collective-permute-start(f32[8,1024]{1,0:T(8,128)S(1)} %next_state.3), channel_id=1, source_target_pairs={{0,28},{1,29},{2,30},{3,31},{4,24},{5,25},{6,26},{7,27},{8,20},{9,... | collective-permute-start | bytes 98312 | tf_op jit(solution)/shard_map/ppermute | solution.py:227
  108.0 7.5 %collective-permute-start.28 = (f32[8,1024]{1,0:T(8,128)S(1)}, f32[8,1024]{1,0:T(8,128)S(1)}, u32[]{:S(2)}, u32[]{:S(2)}) collective-permute-start(f32[8,1024]{1,0:T(8,128)S(1)} %next_state.3), channel_id=1, source_target_pairs={{0,30},{1,31},{2,28},{3,29},{4,26},{5,27},{6,24},{7,25},{8,22},{9,... | collective-permute-start | bytes 98312 | tf_op jit(solution)/shard_map/ppermute | solution.py:227
  115.5 1.4 collective-permute-start.29
  122.4 4.4 %collective-permute-start.30 = (f32[8,1024]{1,0:T(8,128)S(1)}, f32[8,1024]{1,0:T(8,128)S(1)}, u32[]{:S(2)}, u32[]{:S(2)}) collective-permute-start(f32[8,1024]{1,0:T(8,128)S(1)} %first_pass.6), channel_id=1, source_target_pairs={{0,2},{1,3},{2,0},{3,1},{4,6},{5,7},{6,4},{7,5},{8,10},{9,11},{10,... | collective-permute-start | bytes 98312 | tf_op jit(solution)/shard_map/ppermute | solution.py:227
  122.5 5.6 %collective-permute-start.31 = (f32[8,1024]{1,0:T(8,128)S(1)}, f32[8,1024]{1,0:T(8,128)S(1)}, u32[]{:S(2)}, u32[]{:S(2)}) collective-permute-start(f32[8,1024]{1,0:T(8,128)S(1)} %first_pass.6), channel_id=1, source_target_pairs={{0,4},{1,5},{2,6},{3,7},{4,0},{5,1},{6,2},{7,3},{8,12},{9,13},{10,... | collective-permute-start | bytes 98312 | tf_op jit(solution)/shard_map/ppermute | solution.py:227
  125.0 5.7 %collective-permute-start.32 = (f32[8,1024]{1,0:T(8,128)S(1)}, f32[8,1024]{1,0:T(8,128)S(1)}, u32[]{:S(2)}, u32[]{:S(2)}) collective-permute-start(f32[8,1024]{1,0:T(8,128)S(1)} %first_pass.6), channel_id=1, source_target_pairs={{0,6},{1,7},{2,4},{3,5},{4,2},{5,3},{6,0},{7,1},{8,14},{9,15},{10,... | collective-permute-start | bytes 98312 | tf_op jit(solution)/shard_map/ppermute | solution.py:227
  130.7 1.4 collective-permute-start.33
  139.1 4.4 %collective-permute-start.35 = (f32[2,8,128]{2,1,0:T(8,128)S(1)}, f32[2,8,128]{2,1,0:T(8,128)S(1)}, u32[]{:S(2)}, u32[]{:S(2)}) collective-permute-start(f32[2,8,128]{2,1,0:T(8,128)S(1)} %add.14.refs_0_), channel_id=1, source_target_pairs={{0,2},{1,3},{2,0},{3,1},{4,6},{5,7},{6,4},{7,5},{8,10},{9,11},{10,... | collective-permute-start | bytes 24584 | tf_op jit(solution)/shard_map/ppermute | solution.py:227
  139.1 4.6 %collective-permute-start.36 = (f32[2,8,128]{2,1,0:T(8,128)S(1)}, f32[2,8,128]{2,1,0:T(8,128)S(1)}, u32[]{:S(2)}, u32[]{:S(2)}) collective-permute-start(f32[2,8,128]{2,1,0:T(8,128)S(1)} %add.14.refs_0_), channel_id=1, source_target_pairs={{0,4},{1,5},{2,6},{3,7},{4,0},{5,1},{6,2},{7,3},{8,12},{9,13},{10,... | collective-permute-start | bytes 24584 | tf_op jit(solution)/shard_map/ppermute | solution.py:227
  141.5 5.4 %collective-permute-start.37 = (f32[2,8,128]{2,1,0:T(8,128)S(1)}, f32[2,8,128]{2,1,0:T(8,128)S(1)}, u32[]{:S(2)}, u32[]{:S(2)}) collective-permute-start(f32[2,8,128]{2,1,0:T(8,128)S(1)} %add.14.refs_0_), channel_id=1, source_target_pairs={{0,6},{1,7},{2,4},{3,5},{4,2},{5,3},{6,0},{7,1},{8,14},{9,15},{10,... | collective-permute-start | bytes 24584 | tf_op jit(solution)/shard_map/ppermute | solution.py:227
  147.1 6.8 %collective-permute-start.38 = (f32[8,1024]{1,0:T(8,128)S(1)}, f32[8,1024]{1,0:T(8,128)S(1)}, u32[]{:S(2)}, u32[]{:S(2)}) collective-permute-start(f32[8,1024]{1,0:T(8,128)S(1)} %next_state.4), channel_id=1, source_target_pairs={{0,8},{1,9},{2,10},{3,11},{4,12},{5,13},{6,14},{7,15},{8,0},{9,1},... | collective-permute-start | bytes 98312 | tf_op jit(solution)/shard_map/ppermute | solution.py:227
  148.6 5.3 %collective-permute-start.39 = (f32[8,1024]{1,0:T(8,128)S(1)}, f32[8,1024]{1,0:T(8,128)S(1)}, u32[]{:S(2)}, u32[]{:S(2)}) collective-permute-start(f32[8,1024]{1,0:T(8,128)S(1)} %next_state.4), channel_id=1, source_target_pairs={{0,10},{1,11},{2,8},{3,9},{4,14},{5,15},{6,12},{7,13},{8,2},{9,3},... | collective-permute-start | bytes 98312 | tf_op jit(solution)/shard_map/ppermute | solution.py:227
  148.6 5.7 %collective-permute-start.40 = (f32[8,1024]{1,0:T(8,128)S(1)}, f32[8,1024]{1,0:T(8,128)S(1)}, u32[]{:S(2)}, u32[]{:S(2)}) collective-permute-start(f32[8,1024]{1,0:T(8,128)S(1)} %next_state.4), channel_id=1, source_target_pairs={{0,12},{1,13},{2,14},{3,15},{4,8},{5,9},{6,10},{7,11},{8,4},{9,5},... | collective-permute-start | bytes 98312 | tf_op jit(solution)/shard_map/ppermute | solution.py:227
  152.0 6.6 %collective-permute-start.41 = (f32[8,1024]{1,0:T(8,128)S(1)}, f32[8,1024]{1,0:T(8,128)S(1)}, u32[]{:S(2)}, u32[]{:S(2)}) collective-permute-start(f32[8,1024]{1,0:T(8,128)S(1)} %next_state.4), channel_id=1, source_target_pairs={{0,14},{1,15},{2,12},{3,13},{4,10},{5,11},{6,8},{7,9},{8,6},{9,7},... | collective-permute-start | bytes 98312 | tf_op jit(solution)/shard_map/ppermute | solution.py:227
  158.7 1.4 collective-permute-start.42
  165.5 4.4 %collective-permute-start.43 = (f32[8,1024]{1,0:T(8,128)S(1)}, f32[8,1024]{1,0:T(8,128)S(1)}, u32[]{:S(2)}, u32[]{:S(2)}) collective-permute-start(f32[8,1024]{1,0:T(8,128)S(1)} %first_pass.7), channel_id=1, source_target_pairs={{0,2},{1,3},{2,0},{3,1},{4,6},{5,7},{6,4},{7,5},{8,10},{9,11},{10,... | collective-permute-start | bytes 98312 | tf_op jit(solution)/shard_map/ppermute | solution.py:227
  165.6 5.4 %collective-permute-start.44 = (f32[8,1024]{1,0:T(8,128)S(1)}, f32[8,1024]{1,0:T(8,128)S(1)}, u32[]{:S(2)}, u32[]{:S(2)}) collective-permute-start(f32[8,1024]{1,0:T(8,128)S(1)} %first_pass.7), channel_id=1, source_target_pairs={{0,4},{1,5},{2,6},{3,7},{4,0},{5,1},{6,2},{7,3},{8,12},{9,13},{10,... | collective-permute-start | bytes 98312 | tf_op jit(solution)/shard_map/ppermute | solution.py:227
  168.0 5.7 %collective-permute-start.45 = (f32[8,1024]{1,0:T(8,128)S(1)}, f32[8,1024]{1,0:T(8,128)S(1)}, u32[]{:S(2)}, u32[]{:S(2)}) collective-permute-start(f32[8,1024]{1,0:T(8,128)S(1)} %first_pass.7), channel_id=1, source_target_pairs={{0,6},{1,7},{2,4},{3,5},{4,2},{5,3},{6,0},{7,1},{8,14},{9,15},{10,... | collective-permute-start | bytes 98312 | tf_op jit(solution)/shard_map/ppermute | solution.py:227
  173.7 1.4 collective-permute-start.46
  182.1 4.4 %collective-permute-start.48 = (f32[2,8,128]{2,1,0:T(8,128)S(1)}, f32[2,8,128]{2,1,0:T(8,128)S(1)}, u32[]{:S(2)}, u32[]{:S(2)}) collective-permute-start(f32[2,8,128]{2,1,0:T(8,128)S(1)} %add.15.refs_0_), channel_id=1, source_target_pairs={{0,2},{1,3},{2,0},{3,1},{4,6},{5,7},{6,4},{7,5},{8,10},{9,11},{10,... | collective-permute-start | bytes 24584 | tf_op jit(solution)/shard_map/ppermute | solution.py:227
  182.1 4.6 %collective-permute-start.49 = (f32[2,8,128]{2,1,0:T(8,128)S(1)}, f32[2,8,128]{2,1,0:T(8,128)S(1)}, u32[]{:S(2)}, u32[]{:S(2)}) collective-permute-start(f32[2,8,128]{2,1,0:T(8,128)S(1)} %add.15.refs_0_), channel_id=1, source_target_pairs={{0,4},{1,5},{2,6},{3,7},{4,0},{5,1},{6,2},{7,3},{8,12},{9,13},{10,... | collective-permute-start | bytes 24584 | tf_op jit(solution)/shard_map/ppermute | solution.py:227
  184.6 5.4 %collective-permute-start.50 = (f32[2,8,128]{2,1,0:T(8,128)S(1)}, f32[2,8,128]{2,1,0:T(8,128)S(1)}, u32[]{:S(2)}, u32[]{:S(2)}) collective-permute-start(f32[2,8,128]{2,1,0:T(8,128)S(1)} %add.15.refs_0_), channel_id=1, source_target_pairs={{0,6},{1,7},{2,4},{3,5},{4,2},{5,3},{6,0},{7,1},{8,14},{9,15},{10,... | collective-permute-start | bytes 24584 | tf_op jit(solution)/shard_map/ppermute | solution.py:227
  (4 other events, 16.9 us)

commit v2 on v1

v2 whole, which is shorter than its diff:
```python
import functools

import jax
import jax.numpy as jnp
from jax import lax
from jax.experimental import pallas as pl
from jax.experimental.pallas import tpu as pltpu
from jax.sharding import PartitionSpec as P


time_step = 0.125
epsilon = 1e-06
squarings = 5
taylor_terms = 12
MIB = 1 << 20
VMEM = pl.BlockSpec(memory_space=pltpu.VMEM)
SMEM = pl.BlockSpec(memory_space=pltpu.SMEM)
ANY = pl.BlockSpec(memory_space=pl.ANY)
LOAD_WIDTH = 256
LOAD_SLOTS = 8
PIECES = 4


def load_kernel(devices, me_ref, a_ref, *refs):
    piece_refs, (slots, sems) = refs[:PIECES], refs[PIECES:]
    _, extent = a_ref.shape
    width = slots.shape[2]
    block = extent // devices
    per_block = block // width
    steps = extent // width
    half = devices // 2
    me = me_ref[0]

    def source(step):
        place = step // per_block
        offset = jnp.where(place < half, 2 * place, 2 * (place - half) + 1)
        owner = jnp.bitwise_xor(me, offset)
        start = owner * block + (step % per_block) * width
        return a_ref.at[:, pl.ds(pl.multiple_of(start, width), width)]

    def copy(step):
        slot = step % LOAD_SLOTS
        return pltpu.make_async_copy(source(step), slots.at[slot], sems.at[slot])

    for step in range(min(LOAD_SLOTS, steps)):
        copy(step).start()

    per_piece = steps // PIECES
    for piece, piece_ref in enumerate(piece_refs):

        @pl.loop(0, per_piece)
        def _(inner):
            step = inner + piece * per_piece
            copy(step).wait()
            turned = slots[step % LOAD_SLOTS].T
            high = turned.astype(jnp.bfloat16)
            place = pl.ds(pl.multiple_of(inner * width, width), width)
            piece_ref[0, place, :] = high
            piece_ref[1, place, :] = (turned - high.astype(jnp.float32)).astype(jnp.bfloat16)

            @pl.when(step + LOAD_SLOTS < steps)
            def _():
                copy(step + LOAD_SLOTS).start()


def load_operator(local_coupling, me, devices):
    rows, extent = local_coupling.shape
    width = min(LOAD_WIDTH, extent // devices)

    return pl.pallas_call(
        functools.partial(load_kernel, devices),
        out_shape=(pltpu.VMEM((2, extent // PIECES, rows), jnp.bfloat16),) * PIECES,
        in_specs=[SMEM, ANY],
        out_specs=(VMEM,) * PIECES,
        scratch_shapes=[
            pltpu.VMEM((LOAD_SLOTS, rows, width), jnp.float32),
            pltpu.SemaphoreType.DMA((LOAD_SLOTS,)),
        ],
        compiler_params=pltpu.CompilerParams(vmem_limit_bytes=12 * MIB),
        cost_estimate=pl.CostEstimate(
            flops=1600 * rows * extent, bytes_accessed=4 * rows * extent, transcendentals=0
        ),
        name="load_operator",
    )(me, local_coupling)


def apply_rows(blocks, places, piece_refs, split_ref, total_ref):
    members, width = blocks[0].shape
    per_piece = piece_refs[0].shape[1] // width
    total_ref[...] = jnp.zeros_like(total_ref)
    for index, (block, place) in enumerate(zip(blocks, places)):
        high = block.astype(jnp.bfloat16).astype(jnp.float32)
        split_ref[index, :members] = high
        split_ref[index, members:] = block - high
    for index, place in enumerate(places):
        piece_ref = piece_refs[place // per_piece]
        inside = pl.ds(place % per_piece * width, width)
        lhs = split_ref[index].astype(jnp.bfloat16)
        total_ref[...] += jnp.dot(
            lhs, piece_ref[0, inside, :], preferred_element_type=jnp.float32
        ) + jnp.dot(lhs, piece_ref[1, inside, :], preferred_element_type=jnp.float32)
    return total_ref[:members] + total_ref[members:]


def inner_product(first, second):
    return jnp.sum(jnp.sum(first * second, axis=0), axis=-1, keepdims=True)


def widened(value):
    return jnp.broadcast_to(value, (value.shape[0], 128))


def first_early(places, *refs):
    count = len(places)
    x_refs, piece_refs = refs[:count], refs[count:-3]
    out_ref, split_ref, total_ref = refs[-3:]
    out_ref[...] = apply_rows(
        [ref[...] for ref in x_refs], places, piece_refs, split_ref, total_ref
    )


def first_near(places, xa_ref, begun_ref, *refs):
    piece_refs, (out_ref, split_ref, total_ref) = refs[:-3], refs[-3:]
    blocks = [xa_ref[place] for place in places]
    out_ref[...] = begun_ref[...] + apply_rows(blocks, places, piece_refs, split_ref, total_ref)


def first_far(xa_ref, xb_ref, begun_ref, damping_ref, *refs):
    piece_refs, (image_ref, norm_ref, split_ref, total_ref) = refs[:-4], refs[-4:]
    xa, xb = xa_ref[...], xb_ref[...]
    norm = jnp.sqrt(inner_product(xa, xa) + inner_product(xb, xb) + epsilon)
    blocks = list(xb)
    image = begun_ref[...] + apply_rows(
        blocks, range(len(blocks)), piece_refs, split_ref, total_ref
    )
    image_ref[...] = (image - damping_ref[...] * xa[0]) / norm
    norm_ref[...] = widened(norm)


def second_early(places, xa_ref, norm_ref, *refs):
    count = len(places)
    w_refs, piece_refs = refs[:count], refs[count:-4]
    out_ref, estimate_ref, split_ref, total_ref = refs[-4:]
    q = [xa_ref[place] / norm_ref[:, :1] for place in places]
    w = [ref[...] for ref in w_refs]

    def inner(first, second):
        return sum(jnp.sum(x * y, axis=-1, keepdims=True) for x, y in zip(first, second))

    estimate = inner(q, w) / (inner(q, q) + epsilon)
    blocks = [x - estimate * y for x, y in zip(w, q)]
    out_ref[...] = apply_rows(blocks, places, piece_refs, split_ref, total_ref)
    estimate_ref[...] = widened(estimate)


def second_near(places, xa_ref, wa_ref, norm_ref, begun_ref, estimate_ref, *refs):
    piece_refs, (out_ref, split_ref, total_ref) = refs[:-3], refs[-3:]
    norm, estimate = norm_ref[:, :1], estimate_ref[:, :1]
    blocks = [wa_ref[place] - estimate * (xa_ref[place] / norm) for place in places]
    out_ref[...] = begun_ref[...] + apply_rows(blocks, places, piece_refs, split_ref, total_ref)


def second_far(
    xa_ref, xb_ref, wa_ref, wb_ref, norm_ref, begun_ref, estimate_ref, damping_ref, *refs
):
    piece_refs, refs = refs[:-5], refs[-5:]
    partial_ref, scalars_ref, basis_ref, split_ref, total_ref = refs
    wa, wb = wa_ref[...], wb_ref[...]
    norm, estimate = norm_ref[:, :1], estimate_ref[:, :1]
    qa, qb = xa_ref[...] / norm[None], xb_ref[...] / norm[None]
    blocks = list(wb - estimate[None] * qb)
    image = begun_ref[...] + apply_rows(
        blocks, range(len(blocks)), piece_refs, split_ref, total_ref
    )
    first = inner_product(qa, wa) + inner_product(qb, wb)
    ra, rb = wa - first[None] * qa, wb - first[None] * qb
    length = jnp.sqrt(inner_product(ra, ra) + inner_product(rb, rb) + epsilon)
    damping = damping_ref[...]
    image = image + (estimate - first) * (wa[0] + damping * qa[0])
    second = ra[0] / length
    image = image / length - damping * second
    for row, own in ((0, qa[0]), (1, second)):
        partial_ref[row] = widened(jnp.sum(own * image, axis=-1, keepdims=True))
        basis_ref[row] = own
    for row, value in enumerate((norm, first, length)):
        scalars_ref[row] = widened(value)


def exponential(step_size, h00, h01, h10, h11):
    scale = 1.0 / 2.0**squarings
    s00, s01 = step_size * h00 * scale, step_size * h01 * scale
    s10, s11 = step_size * h10 * scale, step_size * h11 * scale
    one, zero = jnp.ones_like(h00), jnp.zeros_like(h00)
    r00, r01, r02, r10, r11, r12 = one, zero, zero, zero, one, zero
    for degree in range(taylor_terms, 0, -1):
        part = 1.0 / degree
        r00, r01, r02, r10, r11, r12 = (
            one + (s00 * r00 + s01 * r10) * part,
            (s00 * r01 + s01 * r11) * part,
            (s00 * r02 + s01 * r12 + scale) * part,
            (s10 * r00 + s11 * r10) * part,
            one + (s10 * r01 + s11 * r11) * part,
            (s10 * r02 + s11 * r12) * part,
        )
    for _ in range(squarings):
        r00, r01, r02, r10, r11, r12 = (
            r00 * r00 + r01 * r10,
            r00 * r01 + r01 * r11,
            r00 * r02 + r01 * r12 + r02,
            r10 * r00 + r11 * r10,
            r10 * r01 + r11 * r11,
            r10 * r02 + r11 * r12 + r12,
        )
    return r00, r10, r02, r12


def combined(step_size, partial_refs, scalars_ref, basis_ref):
    inner = partial_refs[0][...]
    for ref in partial_refs[1:]:
        inner = inner + ref[...]
    norm, first, length = scalars_ref[0], scalars_ref[1], scalars_ref[2]
    e0, e1, f0, f1 = exponential(step_size, first, inner[0], length, inner[1])

    def spread(value):
        return value[:, :1]

    carried = basis_ref[0] * spread(norm * e0) + basis_ref[1] * spread(norm * e1)
    forced = basis_ref[0] * spread(step_size * norm * f0) + basis_ref[1] * spread(
        step_size * norm * f1
    )
    return carried, forced


def start_kernel(sums, members, counts_ref, *refs):
    partial_refs, (scalars_ref, basis_ref, state_ref, local_ref) = refs[:sums], refs[sums:]
    step_size = counts_ref[0].astype(jnp.float32) * time_step
    carried, forced = combined(step_size, partial_refs, scalars_ref, basis_ref)
    local_ref[...] = forced[members:]
    state_ref[...] = carried[:members] + forced[members:]


def next_kernel(sums, counts_ref, *refs):
    partial_refs, (scalars_ref, basis_ref, local_ref, state_ref) = refs[:sums], refs[sums:]
    step_size = counts_ref[0].astype(jnp.float32) * time_step
    carried, _ = combined(step_size, partial_refs, scalars_ref, basis_ref)
    state_ref[...] = carried + local_ref[...]


def permuted(array, tm_change, row_change):
    sections, devices = lax.axis_size("tm"), lax.axis_size("row")
    pairs = [
        (s * devices + r, (s ^ tm_change) * devices + (r ^ row_change))
        for s in range(sections)
        for r in range(devices)
    ]
    return lax.ppermute(array, ("tm", "row"), pairs)


def scattered(array, tm_change=0):
    devices = lax.axis_size("row")
    arrived = {0: array}
    for change in reversed(range(0 if tm_change else 2, devices, 2)):
        arrived[change] = permuted(array, tm_change, change)
    return [arrived[change] for change in range(0, devices, 2)]


def gathered(own, tm_change=0):
    blocks = scattered(own, tm_change)
    near = jnp.stack(blocks)
    return blocks, near, permuted(near, 0, 1)


def summed(partial):
    pair = partial + permuted(partial, 0, 1)
    return scattered(pair)


def on_device(coupling, damping, forcing, initial, counts):
    local_coupling = coupling[0]
    local_forcing = forcing[0]
    members, rows = initial.shape
    extent = local_coupling.shape[1]
    devices = lax.axis_size("row")
    sections = lax.axis_size("tm")
    slab_index = lax.axis_index("tm")
    me = lax.axis_index("row").astype(jnp.int32).reshape(1)

    operator = load_operator(local_coupling, me, devices)

    params = pltpu.CompilerParams(vmem_limit_bytes=8 * MIB)
    near_pieces, far_pieces = operator[: PIECES // 2], operator[PIECES // 2 :]

    def part_pass(kernel, outs, *inputs):
        batch = outs[0][-2]
        return pl.pallas_call(
            kernel,
            out_shape=tuple(jax.ShapeDtypeStruct(shape, jnp.float32) for shape in outs),
            in_specs=[VMEM] * len(inputs),
            out_specs=(VMEM,) * len(outs),
            scratch_shapes=[
                pltpu.VMEM((devices // 2, 2 * batch, rows), jnp.float32),
                pltpu.VMEM((2 * batch, rows), jnp.float32),
            ],
            compiler_params=params,
            cost_estimate=pl.CostEstimate(
                flops=16 * rows * extent, bytes_accessed=rows * extent, transcendentals=0
            ),
        )(*inputs)

    def krylov_step(own, finish, tm_change=0):
        batch = own.shape[0]
        block, lane = (batch, rows), (batch, 128)
        places = range(devices // 2)
        early = [places[-1], places[-2] if tm_change else 0]
        late = [place for place in places if place not in early]
        blocks, xa, xb = gathered(own, tm_change)
        (begun,) = part_pass(
            functools.partial(first_early, early), (block,),
            *[blocks[place] for place in early], *near_pieces,
        )
        (begun,) = part_pass(functools.partial(first_near, late), (block,), xa, begun, *near_pieces)
        image, norm = part_pass(first_far, (block, lane), xa, xb, begun, damping, *far_pieces)
        early = [places[-1], 0]
        late = [place for place in places if place not in early]
        blocks, wa, wb = gathered(image)
        begun, estimate = part_pass(
            functools.partial(second_early, early), (block, lane),
            xa, norm, *[blocks[place] for place in early], *near_pieces,
        )
        (begun,) = part_pass(
            functools.partial(second_near, late), (block,),
            xa, wa, norm, begun, estimate, *near_pieces,
        )
        partial, scalars, basis = part_pass(
            second_far, ((2, *lane), (3, *lane), (2, *block)),
            xa, xb, wa, wb, norm, begun, estimate, damping, *far_pieces,
        )
        return finish(summed(partial), scalars, basis)

    small = jax.ShapeDtypeStruct((members, rows), jnp.float32)

    def start(parts, scalars, basis):
        return pl.pallas_call(
            functools.partial(start_kernel, len(parts), members),
            out_shape=(small, small),
            in_specs=[SMEM] + [VMEM] * (len(parts) + 2),
            out_specs=(VMEM, VMEM),
            compiler_params=params,
            name="start_state",
        )(counts, *parts, scalars, basis)

    def follow(parts, scalars, basis):
        return pl.pallas_call(
            functools.partial(next_kernel, len(parts)),
            out_shape=small,
            in_specs=[SMEM] + [VMEM] * (len(parts) + 3),
            out_specs=VMEM,
            compiler_params=params,
            name="next_state",
        )(counts, *parts, scalars, basis, local)

    own = jnp.concatenate([initial, local_forcing], axis=0)
    state, local = krylov_step(own, start)
    result = state
    for section in range(1, sections):
        state = krylov_step(state, follow, (section - 1) ^ section)
        result = jnp.where(slab_index == section, state, result)
    return result[None]


def solution(mesh):
    placed = (P("tm", "row", None), P("tm", "row"), P("tm", None, "row"), P(None, "row"), P("tm"))
    return jax.shard_map(
        on_device, mesh=mesh, in_specs=placed, out_specs=P("tm", None, "row"), check_vma=False
    )
```

time: 191 us -> 166 us (0.87)
  waiting for transfers between devices: 63.2 us -> 46.7 us
  Pallas kernels: 61.9 us -> 55.1 us
    ppermute x51, waiting for transfers between devices: 63.2 us -> 46.7 us  [permuted(): return lax.ppermute(array, ('tm', 'row'), pairs)]
    pallas_call x12 -> x28, Pallas kernels: 48.6 us -> 41.9 us  [the longest x24 41.3 us: part_pass(): pl.pallas_call(kernel, out_shape=tuple((jax.ShapeDtypeStruct(shape, jnp.f...]
  transfers between devices with their start and end apart: 51 -> 51, of which waited for: 35 -> 34; matrix products, arithmetic and copies ran while one was open for 0% -> 0% of each run, Pallas kernels for 7% -> 21%
where the time goes in v2:
time: 166 us
  starting transfers between devices  62 us (37%)
  Pallas kernels  55.1 us (33%)
  waiting for transfers between devices  46.7 us (28%)
    ppermute x51, starting transfers between devices, permuted(): return lax.ppermute(array, ('tm', 'row'), pairs)  62 us
    ppermute x51, waiting for transfers between devices, permuted(): return lax.ppermute(array, ('tm', 'row'), pairs)  46.7 us
    pallas_call x24, Pallas kernels, part_pass(): pl.pallas_call(kernel, out_shape=tuple((jax.ShapeDtypeStruct(shape, jnp.f...  41.3 us
    pallas_call x1, Pallas kernels, load_operator(): pl.pallas_call(functools.partial(load_kernel, devices), out_shape=(pltpu....  13.3 us
  transfers between devices with their start and end apart: 51, of which 34 were waited for; matrix products, arithmetic and copies ran while one was open for 0% of the time, Pallas kernels for 21%

profile of v2, /device:TPU:0, one launch (start us, length us, event | category | flops | bytes accessed | tf_op | source)
XLA Modules:
  0.0 166.2 jit_solution(9242419763168171681)
XLA Ops:
  0.8 5.1 %collective-permute-start.2 = (f32[16,1024]{1,0:T(8,128)S(1)}, f32[16,1024]{1,0:T(8,128)S(1)}, u32[]{:S(2)}, u32[]{:S(2)}) collective-permute-start(f32[16,1024]{1,0:T(8,128)S(1)} %get-tuple-element.74.refs_1_), channel_id=1, source_target_pairs={{0,6},{1,7},{2,4},{3,5},{4,2},{5,3},{6,0},{7,1},{8,14},{9,15},{10,... | collective-permute-start | bytes 196616 | tf_op jit(solution)/shard_map/ppermute | solution.py:256
  6.6 2.2 %collective-permute-done.2.refs_0_ = f32[16,1024]{1,0:T(8,128)S(1)} collective-permute-done((f32[16,1024]{1,0:T(8,128)S(1)}, f32[16,1024]{1,0:T(8,128)S(1)}, u32[]{:S(2)}, u32[]{:S(2)}) %collective-permute-start.2) | collective-permute-done | bytes 65568 | tf_op jit(solution)/shard_map/ppermute | solution.py:256
  8.8 1.8 %collective-permute-done = f32[16,1024]{1,0:T(8,128)S(1)} collective-permute-done((f32[16,1024]{1,0:T(8,128)S(1)}, f32[16,1024]{1,0:T(8,128)S(1)}, u32[]{:S(2)}, u32[]{:S(2)}) %collective-permute-start) | collective-permute-done | bytes 65568 | tf_op jit(solution)/shard_map/ppermute | solution.py:256
  11.7 13.3 %load_operator.1 = (bf16[2,2048,1024]{2,1,0:T(8,128)(2,1)S(1)}, bf16[2,2048,1024]{2,1,0:T(8,128)(2,1)S(1)}, bf16[2,2048,1024]{2,1,0:T(8,128)(2,1)S(1)}, bf16[2,2048,1024]{2,1,0:T(8,128)(2,1)S(1)}) custom-call(s32[1]{0:T(128)} %bitcast.5.me_ref, f32[1024,8192]{1,0:T(8,128)} %bitcast.70), custom_call_target="tpu_custom_call" | custom-call | flops 13421772800 | bytes 33554432 | tf_op jit(solution)/shard_map/load_operator/pallas_call | solution.py:70
  27.8 2.8 %shard_map.57 = (f32[16,1024]{1,0:T(8,128)S(1)}, f32[16,128]{1,0:T(8,128)S(1)}) custom-call(f32[4,16,1024]{2,1,0:T(8,128)S(1)} %pad_maximum_fusion.xa_ref, f32[4,16,1024]{2,1,0:T(8,128)S(1)} %collective-permute-done.3.xb_ref, f32[16,1024]{1,0:T(8,128)S(1)} %shard_map.56.begun_ref, f32[1,1024]{1,0:T(1,128)S(1)} %copy-done, ...), custom_call_target="tpu_custom_call" | custom-call | flops 134217728 | bytes 8388608 | tf_op jit(solution)/shard_map/pallas_call | solution.py:295
  30.6 2.9 %collective-permute-start.6 = (f32[16,1024]{1,0:T(8,128)S(1)}, f32[16,1024]{1,0:T(8,128)S(1)}, u32[]{:S(2)}, u32[]{:S(2)}) collective-permute-start(f32[16,1024]{1,0:T(8,128)S(1)} %get-tuple-element.43.refs_1_), channel_id=1, source_target_pairs={{0,6},{1,7},{2,4},{3,5},{4,2},{5,3},{6,0},{7,1},{8,14},{9,15},{10,... | collective-permute-start | bytes 196616 | tf_op jit(solution)/shard_map/ppermute | solution.py:256
  33.4 1.5 collective-permute-start.5
  35.0 2.4 %collective-permute-done.6.refs_0_ = f32[16,1024]{1,0:T(8,128)S(1)} collective-permute-done((f32[16,1024]{1,0:T(8,128)S(1)}, f32[16,1024]{1,0:T(8,128)S(1)}, u32[]{:S(2)}, u32[]{:S(2)}) %collective-permute-start.6) | collective-permute-done | bytes 65568 | tf_op jit(solution)/shard_map/ppermute | solution.py:256
  37.3 2.2 %collective-permute-done.4 = f32[16,1024]{1,0:T(8,128)S(1)} collective-permute-done((f32[16,1024]{1,0:T(8,128)S(1)}, f32[16,1024]{1,0:T(8,128)S(1)}, u32[]{:S(2)}, u32[]{:S(2)}) %collective-permute-start.4) | collective-permute-done | bytes 65568 | tf_op jit(solution)/shard_map/ppermute | solution.py:256
  40.4 1.6 shard_map.58
  42.0 1.6 shard_map.59.begun_ref
  43.6 3.1 %shard_map.60 = (f32[2,16,128]{2,1,0:T(8,128)S(1)}, f32[3,16,128]{2,1,0:T(8,128)S(1)}, f32[2,16,1024]{2,1,0:T(8,128)S(1)}) custom-call(f32[4,16,1024]{2,1,0:T(8,128)S(1)} %pad_maximum_fusion.xa_ref, f32[4,16,1024]{2,1,0:T(8,128)S(1)} %collective-permute-done.3.xb_ref, f32[4,16,1024]{2,1,0:T(8,128)S(1)} %pad_maximum_fusion.1.wa_ref, ...), custom_call_target="tpu_custom_call" | custom-call | flops 134217728 | bytes 8388608 | tf_op jit(solution)/shard_map/pallas_call | solution.py:295
  52.7 2.3 %collective-permute-done.11.refs_3_ = f32[2,16,128]{2,1,0:T(8,128)S(1)} collective-permute-done((f32[2,16,128]{2,1,0:T(8,128)S(1)}, f32[2,16,128]{2,1,0:T(8,128)S(1)}, u32[]{:S(2)}, u32[]{:S(2)}) %collective-permute-start.11) | collective-permute-done | bytes 16416 | tf_op jit(solution)/shard_map/ppermute | solution.py:256
  55.1 2.1 %collective-permute-start.14 = (f32[8,1024]{1,0:T(8,128)S(1)}, f32[8,1024]{1,0:T(8,128)S(1)}, u32[]{:S(2)}, u32[]{:S(2)}) collective-permute-start(f32[8,1024]{1,0:T(8,128)S(1)} %get-tuple-element.50), channel_id=1, source_target_pairs={{0,12},{1,13},{2,14},{3,15},{4,8},{5,9},{6,10},{7,11},{8,4},{9,5},... | collective-permute-start | bytes 98312 | tf_op jit(solution)/shard_map/ppermute | solution.py:256
  61.7 2.2 %collective-permute-done.15.refs_0_ = f32[8,1024]{1,0:T(8,128)S(1)} collective-permute-done((f32[8,1024]{1,0:T(8,128)S(1)}, f32[8,1024]{1,0:T(8,128)S(1)}, u32[]{:S(2)}, u32[]{:S(2)}) %collective-permute-start.15) | collective-permute-done | bytes 32800 | tf_op jit(solution)/shard_map/ppermute | solution.py:256
  67.5 2.3 %shard_map.63 = (f32[8,1024]{1,0:T(8,128)S(1)}, f32[8,128]{1,0:T(8,128)S(1)}) custom-call(f32[4,8,1024]{2,1,0:T(8,128)S(1)} %pad_maximum_fusion.2.xa_ref, f32[4,8,1024]{2,1,0:T(8,128)S(1)} %collective-permute-done.16.xb_ref, f32[8,1024]{1,0:T(8,128)S(1)} %shard_map.62.begun_ref, f32[1,1024]{1,0:T(1,128)S(1)} %copy-done, ...), custom_call_target="tpu_custom_call" | custom-call | flops 134217728 | bytes 8388608 | tf_op jit(solution)/shard_map/pallas_call | solution.py:295
  69.8 2.3 %collective-permute-start.19 = (f32[8,1024]{1,0:T(8,128)S(1)}, f32[8,1024]{1,0:T(8,128)S(1)}, u32[]{:S(2)}, u32[]{:S(2)}) collective-permute-start(f32[8,1024]{1,0:T(8,128)S(1)} %get-tuple-element.51.refs_1_), channel_id=1, source_target_pairs={{0,6},{1,7},{2,4},{3,5},{4,2},{5,3},{6,0},{7,1},{8,14},{9,15},{10,... | collective-permute-start | bytes 98312 | tf_op jit(solution)/shard_map/ppermute | solution.py:256
  72.1 2.1 %collective-permute-start.18 = (f32[8,1024]{1,0:T(8,128)S(1)}, f32[8,1024]{1,0:T(8,128)S(1)}, u32[]{:S(2)}, u32[]{:S(2)}) collective-permute-start(f32[8,1024]{1,0:T(8,128)S(1)} %get-tuple-element.51.refs_1_), channel_id=1, source_target_pairs={{0,4},{1,5},{2,6},{3,7},{4,0},{5,1},{6,2},{7,3},{8,12},{9,13},{10,... | collective-permute-start | bytes 98312 | tf_op jit(solution)/shard_map/ppermute | solution.py:256
  74.2 1.5 collective-permute-done.19.refs_0_
  79.6 2.4 %shard_map.66 = (f32[2,8,128]{2,1,0:T(8,128)S(1)}, f32[3,8,128]{2,1,0:T(8,128)S(1)}, f32[2,8,1024]{2,1,0:T(8,128)S(1)}) custom-call(f32[4,8,1024]{2,1,0:T(8,128)S(1)} %pad_maximum_fusion.2.xa_ref, f32[4,8,1024]{2,1,0:T(8,128)S(1)} %collective-permute-done.16.xb_ref, f32[4,8,1024]{2,1,0:T(8,128)S(1)} %pad_maximum_fusion.3.wa_ref, ...), custom_call_target="tpu_custom_call" | custom-call | flops 134217728 | bytes 8388608 | tf_op jit(solution)/shard_map/pallas_call | solution.py:295
  83.4 2.0 %collective-permute-start.22 = (f32[2,8,128]{2,1,0:T(8,128)S(1)}, f32[2,8,128]{2,1,0:T(8,128)S(1)}, u32[]{:S(2)}, u32[]{:S(2)}) collective-permute-start(f32[2,8,128]{2,1,0:T(8,128)S(1)} %add.13.refs_0_), channel_id=1, source_target_pairs={{0,2},{1,3},{2,0},{3,1},{4,6},{5,7},{6,4},{7,5},{8,10},{9,11},{10,... | collective-permute-start | bytes 24584 | tf_op jit(solution)/shard_map/ppermute | solution.py:256
  85.8 2.0 %collective-permute-start.24 = (f32[2,8,128]{2,1,0:T(8,128)S(1)}, f32[2,8,128]{2,1,0:T(8,128)S(1)}, u32[]{:S(2)}, u32[]{:S(2)}) collective-permute-start(f32[2,8,128]{2,1,0:T(8,128)S(1)} %add.13.refs_0_), channel_id=1, source_target_pairs={{0,6},{1,7},{2,4},{3,5},{4,2},{5,3},{6,0},{7,1},{8,14},{9,15},{10,... | collective-permute-start | bytes 24584 | tf_op jit(solution)/shard_map/ppermute | solution.py:256
  87.8 2.2 %collective-permute-done.23.refs_2_ = f32[2,8,128]{2,1,0:T(8,128)S(1)} collective-permute-done((f32[2,8,128]{2,1,0:T(8,128)S(1)}, f32[2,8,128]{2,1,0:T(8,128)S(1)}, u32[]{:S(2)}, u32[]{:S(2)}) %collective-permute-start.23) | collective-permute-done | bytes 8224 | tf_op jit(solution)/shard_map/ppermute | solution.py:256
  91.4 1.7 %collective-permute-start.27 = (f32[8,1024]{1,0:T(8,128)S(1)}, f32[8,1024]{1,0:T(8,128)S(1)}, u32[]{:S(2)}, u32[]{:S(2)}) collective-permute-start(f32[8,1024]{1,0:T(8,128)S(1)} %next_state.3), channel_id=1, source_target_pairs={{0,28},{1,29},{2,30},{3,31},{4,24},{5,25},{6,26},{7,27},{8,20},{9,... | collective-permute-start | bytes 98312 | tf_op jit(solution)/shard_map/ppermute | solution.py:256
  93.1 2.4 %collective-permute-start.28 = (f32[8,1024]{1,0:T(8,128)S(1)}, f32[8,1024]{1,0:T(8,128)S(1)}, u32[]{:S(2)}, u32[]{:S(2)}) collective-permute-start(f32[8,1024]{1,0:T(8,128)S(1)} %next_state.3), channel_id=1, source_target_pairs={{0,30},{1,31},{2,28},{3,29},{4,26},{5,27},{6,24},{7,25},{8,22},{9,... | collective-permute-start | bytes 98312 | tf_op jit(solution)/shard_map/ppermute | solution.py:256
  97.0 2.1 %collective-permute-start.26 = (f32[8,1024]{1,0:T(8,128)S(1)}, f32[8,1024]{1,0:T(8,128)S(1)}, u32[]{:S(2)}, u32[]{:S(2)}) collective-permute-start(f32[8,1024]{1,0:T(8,128)S(1)} %next_state.3), channel_id=1, source_target_pairs={{0,26},{1,27},{2,24},{3,25},{4,30},{5,31},{6,28},{7,29},{8,18},{9,... | collective-permute-start | bytes 98312 | tf_op jit(solution)/shard_map/ppermute | solution.py:256
  99.1 1.6 collective-permute-done.28.refs_0_
  100.6 2.0 %collective-permute-done.26 = f32[8,1024]{1,0:T(8,128)S(1)} collective-permute-done((f32[8,1024]{1,0:T(8,128)S(1)}, f32[8,1024]{1,0:T(8,128)S(1)}, u32[]{:S(2)}, u32[]{:S(2)}) %collective-permute-start.26) | collective-permute-done | bytes 32800 | tf_op jit(solution)/shard_map/ppermute | solution.py:256
  105.2 2.3 %shard_map.69 = (f32[8,1024]{1,0:T(8,128)S(1)}, f32[8,128]{1,0:T(8,128)S(1)}) custom-call(f32[4,8,1024]{2,1,0:T(8,128)S(1)} %pad_maximum_fusion.4.xa_ref, f32[4,8,1024]{2,1,0:T(8,128)S(1)} %collective-permute-done.29.xb_ref, f32[8,1024]{1,0:T(8,128)S(1)} %shard_map.68.begun_ref, f32[1,1024]{1,0:T(1,128)S(1)} %copy-done, ...), custom_call_target="tpu_custom_call" | custom-call | flops 134217728 | bytes 8388608 | tf_op jit(solution)/shard_map/pallas_call | solution.py:295
  107.5 2.3 %collective-permute-start.32 = (f32[8,1024]{1,0:T(8,128)S(1)}, f32[8,1024]{1,0:T(8,128)S(1)}, u32[]{:S(2)}, u32[]{:S(2)}) collective-permute-start(f32[8,1024]{1,0:T(8,128)S(1)} %get-tuple-element.59.refs_1_), channel_id=1, source_target_pairs={{0,6},{1,7},{2,4},{3,5},{4,2},{5,3},{6,0},{7,1},{8,14},{9,15},{10,... | collective-permute-start | bytes 98312 | tf_op jit(solution)/shard_map/ppermute | solution.py:256
  109.8 2.1 %collective-permute-start.31 = (f32[8,1024]{1,0:T(8,128)S(1)}, f32[8,1024]{1,0:T(8,128)S(1)}, u32[]{:S(2)}, u32[]{:S(2)}) collective-permute-start(f32[8,1024]{1,0:T(8,128)S(1)} %get-tuple-element.59.refs_1_), channel_id=1, source_target_pairs={{0,4},{1,5},{2,6},{3,7},{4,0},{5,1},{6,2},{7,3},{8,12},{9,13},{10,... | collective-permute-start | bytes 98312 | tf_op jit(solution)/shard_map/ppermute | solution.py:256
  111.9 1.6 collective-permute-done.32.refs_0_
  117.3 2.7 %shard_map.72 = (f32[2,8,128]{2,1,0:T(8,128)S(1)}, f32[3,8,128]{2,1,0:T(8,128)S(1)}, f32[2,8,1024]{2,1,0:T(8,128)S(1)}) custom-call(f32[4,8,1024]{2,1,0:T(8,128)S(1)} %pad_maximum_fusion.4.xa_ref, f32[4,8,1024]{2,1,0:T(8,128)S(1)} %collective-permute-done.29.xb_ref, f32[4,8,1024]{2,1,0:T(8,128)S(1)} %pad_maximum_fusion.5.wa_ref, ...), custom_call_target="tpu_custom_call" | custom-call | flops 134217728 | bytes 8388608 | tf_op jit(solution)/shard_map/pallas_call | solution.py:295
  121.3 2.0 %collective-permute-start.35 = (f32[2,8,128]{2,1,0:T(8,128)S(1)}, f32[2,8,128]{2,1,0:T(8,128)S(1)}, u32[]{:S(2)}, u32[]{:S(2)}) collective-permute-start(f32[2,8,128]{2,1,0:T(8,128)S(1)} %add.14.refs_0_), channel_id=1, source_target_pairs={{0,2},{1,3},{2,0},{3,1},{4,6},{5,7},{6,4},{7,5},{8,10},{9,11},{10,... | collective-permute-start | bytes 24584 | tf_op jit(solution)/shard_map/ppermute | solution.py:256
  124.0 1.6 collective-permute-start.37
  125.6 2.2 %collective-permute-done.36.refs_2_ = f32[2,8,128]{2,1,0:T(8,128)S(1)} collective-permute-done((f32[2,8,128]{2,1,0:T(8,128)S(1)}, f32[2,8,128]{2,1,0:T(8,128)S(1)}, u32[]{:S(2)}, u32[]{:S(2)}) %collective-permute-start.36) | collective-permute-done | bytes 8224 | tf_op jit(solution)/shard_map/ppermute | solution.py:256
  127.8 1.6 collective-permute-done.37.refs_3_
  133.9 1.5 collective-permute-start.39
  135.4 2.1 %collective-permute-done.41.refs_0_ = f32[8,1024]{1,0:T(8,128)S(1)} collective-permute-done((f32[8,1024]{1,0:T(8,128)S(1)}, f32[8,1024]{1,0:T(8,128)S(1)}, u32[]{:S(2)}, u32[]{:S(2)}) %collective-permute-start.41) | collective-permute-done | bytes 32800 | tf_op jit(solution)/shard_map/ppermute | solution.py:256
  141.2 2.3 %shard_map.75 = (f32[8,1024]{1,0:T(8,128)S(1)}, f32[8,128]{1,0:T(8,128)S(1)}) custom-call(f32[4,8,1024]{2,1,0:T(8,128)S(1)} %pad_maximum_fusion.6.xa_ref, f32[4,8,1024]{2,1,0:T(8,128)S(1)} %collective-permute-done.42.xb_ref, f32[8,1024]{1,0:T(8,128)S(1)} %shard_map.74.begun_ref, f32[1,1024]{1,0:T(1,128)S(1)} %copy-done, ...), custom_call_target="tpu_custom_call" | custom-call | flops 134217728 | bytes 8388608 | tf_op jit(solution)/shard_map/pallas_call | solution.py:295
  143.5 2.3 %collective-permute-start.45 = (f32[8,1024]{1,0:T(8,128)S(1)}, f32[8,1024]{1,0:T(8,128)S(1)}, u32[]{:S(2)}, u32[]{:S(2)}) collective-permute-start(f32[8,1024]{1,0:T(8,128)S(1)} %get-tuple-element.66.refs_1_), channel_id=1, source_target_pairs={{0,6},{1,7},{2,4},{3,5},{4,2},{5,3},{6,0},{7,1},{8,14},{9,15},{10,... | collective-permute-start | bytes 98312 | tf_op jit(solution)/shard_map/ppermute | solution.py:256
  145.8 2.1 %collective-permute-start.44 = (f32[8,1024]{1,0:T(8,128)S(1)}, f32[8,1024]{1,0:T(8,128)S(1)}, u32[]{:S(2)}, u32[]{:S(2)}) collective-permute-start(f32[8,1024]{1,0:T(8,128)S(1)} %get-tuple-element.66.refs_1_), channel_id=1, source_target_pairs={{0,4},{1,5},{2,6},{3,7},{4,0},{5,1},{6,2},{7,3},{8,12},{9,13},{10,... | collective-permute-start | bytes 98312 | tf_op jit(solution)/shard_map/ppermute | solution.py:256
  147.9 1.6 collective-permute-done.45.refs_0_
  153.3 2.4 %shard_map.78 = (f32[2,8,128]{2,1,0:T(8,128)S(1)}, f32[3,8,128]{2,1,0:T(8,128)S(1)}, f32[2,8,1024]{2,1,0:T(8,128)S(1)}) custom-call(f32[4,8,1024]{2,1,0:T(8,128)S(1)} %pad_maximum_fusion.6.xa_ref, f32[4,8,1024]{2,1,0:T(8,128)S(1)} %collective-permute-done.42.xb_ref, f32[4,8,1024]{2,1,0:T(8,128)S(1)} %pad_maximum_fusion.7.wa_ref, ...), custom_call_target="tpu_custom_call" | custom-call | flops 134217728 | bytes 8388608 | tf_op jit(solution)/shard_map/pallas_call | solution.py:295
  157.1 2.0 %collective-permute-start.48 = (f32[2,8,128]{2,1,0:T(8,128)S(1)}, f32[2,8,128]{2,1,0:T(8,128)S(1)}, u32[]{:S(2)}, u32[]{:S(2)}) collective-permute-start(f32[2,8,128]{2,1,0:T(8,128)S(1)} %add.15.refs_0_), channel_id=1, source_target_pairs={{0,2},{1,3},{2,0},{3,1},{4,6},{5,7},{6,4},{7,5},{8,10},{9,11},{10,... | collective-permute-start | bytes 24584 | tf_op jit(solution)/shard_map/ppermute | solution.py:256
  160.0 1.5 collective-permute-start.50
  161.5 2.2 %collective-permute-done.49.refs_2_ = f32[2,8,128]{2,1,0:T(8,128)S(1)} collective-permute-done((f32[2,8,128]{2,1,0:T(8,128)S(1)}, f32[2,8,128]{2,1,0:T(8,128)S(1)}, u32[]{:S(2)}, u32[]{:S(2)}) %collective-permute-start.49) | collective-permute-done | bytes 8224 | tf_op jit(solution)/shard_map/ppermute | solution.py:256
  163.7 1.7 %collective-permute-done.50.refs_3_ = f32[2,8,128]{2,1,0:T(8,128)S(1)} collective-permute-done((f32[2,8,128]{2,1,0:T(8,128)S(1)}, f32[2,8,128]{2,1,0:T(8,128)S(1)}, u32[]{:S(2)}, u32[]{:S(2)}) %collective-permute-start.50) | collective-permute-done | bytes 8224 | tf_op jit(solution)/shard_map/ppermute | solution.py:256
  (99 shorter events, 51.4 us)
Async XLA Ops:
  0.8 8.0 %collective-permute-start.2 = (f32[16,1024]{1,0:T(8,128)S(1)}, f32[16,1024]{1,0:T(8,128)S(1)}, u32[]{:S(2)}, u32[]{:S(2)}) collective-permute-start(f32[16,1024]{1,0:T(8,128)S(1)} %get-tuple-element.74.refs_1_), channel_id=1, source_target_pairs={{0,6},{1,7},{2,4},{3,5},{4,2},{5,3},{6,0},{7,1},{8,14},{9,15},{10,... | collective-permute-start | bytes 196616 | tf_op jit(solution)/shard_map/ppermute | solution.py:256
  5.9 4.7 %collective-permute-start = (f32[16,1024]{1,0:T(8,128)S(1)}, f32[16,1024]{1,0:T(8,128)S(1)}, u32[]{:S(2)}, u32[]{:S(2)}) collective-permute-start(f32[16,1024]{1,0:T(8,128)S(1)} %get-tuple-element.74.refs_1_), channel_id=1, source_target_pairs={{0,2},{1,3},{2,0},{3,1},{4,6},{5,7},{6,4},{7,5},{8,10},{9,11},{10,... | collective-permute-start | bytes 196616 | tf_op jit(solution)/shard_map/ppermute | solution.py:256
  5.9 5.6 %collective-permute-start.1 = (f32[16,1024]{1,0:T(8,128)S(1)}, f32[16,1024]{1,0:T(8,128)S(1)}, u32[]{:S(2)}, u32[]{:S(2)}) collective-permute-start(f32[16,1024]{1,0:T(8,128)S(1)} %get-tuple-element.74.refs_1_), channel_id=1, source_target_pairs={{0,4},{1,5},{2,6},{3,7},{4,0},{5,1},{6,2},{7,3},{8,12},{9,13},{10,... | collective-permute-start | bytes 196616 | tf_op jit(solution)/shard_map/ppermute | solution.py:256
  11.6 16.2 %collective-permute-start.3 = (f32[4,16,1024]{2,1,0:T(8,128)S(1)}, f32[4,16,1024]{2,1,0:T(8,128)S(1)}, u32[]{:S(2)}, u32[]{:S(2)}) collective-permute-start(f32[4,16,1024]{2,1,0:T(8,128)S(1)} %pad_maximum_fusion.xa_ref), channel_id=1, source_target_pairs={{0,1},{1,0},{2,3},{3,2},{4,5},{5,4},{6,7},{7,6},{8,9},{9,8},{10,11... | collective-permute-start | bytes 786440 | tf_op jit(solution)/shard_map/ppermute | solution.py:256
  30.6 6.8 %collective-permute-start.6 = (f32[16,1024]{1,0:T(8,128)S(1)}, f32[16,1024]{1,0:T(8,128)S(1)}, u32[]{:S(2)}, u32[]{:S(2)}) collective-permute-start(f32[16,1024]{1,0:T(8,128)S(1)} %get-tuple-element.43.refs_1_), channel_id=1, source_target_pairs={{0,6},{1,7},{2,4},{3,5},{4,2},{5,3},{6,0},{7,1},{8,14},{9,15},{10,... | collective-permute-start | bytes 196616 | tf_op jit(solution)/shard_map/ppermute | solution.py:256
  33.4 6.1 %collective-permute-start.4 = (f32[16,1024]{1,0:T(8,128)S(1)}, f32[16,1024]{1,0:T(8,128)S(1)}, u32[]{:S(2)}, u32[]{:S(2)}) collective-permute-start(f32[16,1024]{1,0:T(8,128)S(1)} %get-tuple-element.43.refs_1_), channel_id=1, source_target_pairs={{0,2},{1,3},{2,0},{3,1},{4,6},{5,7},{6,4},{7,5},{8,10},{9,11},{10,... | collective-permute-start | bytes 196616 | tf_op jit(solution)/shard_map/ppermute | solution.py:256
  33.4 6.8 %collective-permute-start.5 = (f32[16,1024]{1,0:T(8,128)S(1)}, f32[16,1024]{1,0:T(8,128)S(1)}, u32[]{:S(2)}, u32[]{:S(2)}) collective-permute-start(f32[16,1024]{1,0:T(8,128)S(1)} %get-tuple-element.43.refs_1_), channel_id=1, source_target_pairs={{0,4},{1,5},{2,6},{3,7},{4,0},{5,1},{6,2},{7,3},{8,12},{9,13},{10,... | collective-permute-start | bytes 196616 | tf_op jit(solution)/shard_map/ppermute | solution.py:256
  40.3 3.3 %collective-permute-start.7 = (f32[4,16,1024]{2,1,0:T(8,128)S(1)}, f32[4,16,1024]{2,1,0:T(8,128)S(1)}, u32[]{:S(2)}, u32[]{:S(2)}) collective-permute-start(f32[4,16,1024]{2,1,0:T(8,128)S(1)} %pad_maximum_fusion.1.wa_ref), channel_id=1, source_target_pairs={{0,1},{1,0},{2,3},{3,2},{4,5},{5,4},{6,7},{7,6},{8,9},{9,8},{10,11... | collective-permute-start | bytes 786440 | tf_op jit(solution)/shard_map/ppermute | solution.py:256
  46.7 1.3 collective-permute-start.8
  48.0 4.6 %collective-permute-start.10 = (f32[2,16,128]{2,1,0:T(8,128)S(1)}, f32[2,16,128]{2,1,0:T(8,128)S(1)}, u32[]{:S(2)}, u32[]{:S(2)}) collective-permute-start(f32[2,16,128]{2,1,0:T(8,128)S(1)} %add.12.refs_0_), channel_id=1, source_target_pairs={{0,4},{1,5},{2,6},{3,7},{4,0},{5,1},{6,2},{7,3},{8,12},{9,13},{10,... | collective-permute-start | bytes 49160 | tf_op jit(solution)/shard_map/ppermute | solution.py:256
  49.4 5.5 %collective-permute-start.11 = (f32[2,16,128]{2,1,0:T(8,128)S(1)}, f32[2,16,128]{2,1,0:T(8,128)S(1)}, u32[]{:S(2)}, u32[]{:S(2)}) collective-permute-start(f32[2,16,128]{2,1,0:T(8,128)S(1)} %add.12.refs_0_), channel_id=1, source_target_pairs={{0,6},{1,7},{2,4},{3,5},{4,2},{5,3},{6,0},{7,1},{8,14},{9,15},{10,... | collective-permute-start | bytes 49160 | tf_op jit(solution)/shard_map/ppermute | solution.py:256
  50.7 4.2 %collective-permute-start.9 = (f32[2,16,128]{2,1,0:T(8,128)S(1)}, f32[2,16,128]{2,1,0:T(8,128)S(1)}, u32[]{:S(2)}, u32[]{:S(2)}) collective-permute-start(f32[2,16,128]{2,1,0:T(8,128)S(1)} %add.12.refs_0_), channel_id=1, source_target_pairs={{0,2},{1,3},{2,0},{3,1},{4,6},{5,7},{6,4},{7,5},{8,10},{9,11},{10,... | collective-permute-start | bytes 49160 | tf_op jit(solution)/shard_map/ppermute | solution.py:256
  55.1 6.5 %collective-permute-start.14 = (f32[8,1024]{1,0:T(8,128)S(1)}, f32[8,1024]{1,0:T(8,128)S(1)}, u32[]{:S(2)}, u32[]{:S(2)}) collective-permute-start(f32[8,1024]{1,0:T(8,128)S(1)} %get-tuple-element.50), channel_id=1, source_target_pairs={{0,12},{1,13},{2,14},{3,15},{4,8},{5,9},{6,10},{7,11},{8,4},{9,5},... | collective-permute-start | bytes 98312 | tf_op jit(solution)/shard_map/ppermute | solution.py:256
  57.2 6.6 %collective-permute-start.15 = (f32[8,1024]{1,0:T(8,128)S(1)}, f32[8,1024]{1,0:T(8,128)S(1)}, u32[]{:S(2)}, u32[]{:S(2)}) collective-permute-start(f32[8,1024]{1,0:T(8,128)S(1)} %get-tuple-element.50), channel_id=1, source_target_pairs={{0,14},{1,15},{2,12},{3,13},{4,10},{5,11},{6,8},{7,9},{8,6},{9,7},... | collective-permute-start | bytes 98312 | tf_op jit(solution)/shard_map/ppermute | solution.py:256
  58.7 5.1 %collective-permute-start.12 = (f32[8,1024]{1,0:T(8,128)S(1)}, f32[8,1024]{1,0:T(8,128)S(1)}, u32[]{:S(2)}, u32[]{:S(2)}) collective-permute-start(f32[8,1024]{1,0:T(8,128)S(1)} %get-tuple-element.50), channel_id=1, source_target_pairs={{0,8},{1,9},{2,10},{3,11},{4,12},{5,13},{6,14},{7,15},{8,0},{9,1},... | collective-permute-start | bytes 98312 | tf_op jit(solution)/shard_map/ppermute | solution.py:256
  60.2 4.8 %collective-permute-start.13 = (f32[8,1024]{1,0:T(8,128)S(1)}, f32[8,1024]{1,0:T(8,128)S(1)}, u32[]{:S(2)}, u32[]{:S(2)}) collective-permute-start(f32[8,1024]{1,0:T(8,128)S(1)} %get-tuple-element.50), channel_id=1, source_target_pairs={{0,10},{1,11},{2,8},{3,9},{4,14},{5,15},{6,12},{7,13},{8,2},{9,3},... | collective-permute-start | bytes 98312 | tf_op jit(solution)/shard_map/ppermute | solution.py:256
  65.1 2.5 %collective-permute-start.16 = (f32[4,8,1024]{2,1,0:T(8,128)S(1)}, f32[4,8,1024]{2,1,0:T(8,128)S(1)}, u32[]{:S(2)}, u32[]{:S(2)}) collective-permute-start(f32[4,8,1024]{2,1,0:T(8,128)S(1)} %pad_maximum_fusion.2.xa_ref), channel_id=1, source_target_pairs={{0,1},{1,0},{2,3},{3,2},{4,5},{5,4},{6,7},{7,6},{8,9},{9,8},{10,11... | collective-permute-start | bytes 393224 | tf_op jit(solution)/shard_map/ppermute | solution.py:256
  69.8 5.9 %collective-permute-start.19 = (f32[8,1024]{1,0:T(8,128)S(1)}, f32[8,1024]{1,0:T(8,128)S(1)}, u32[]{:S(2)}, u32[]{:S(2)}) collective-permute-start(f32[8,1024]{1,0:T(8,128)S(1)} %get-tuple-element.51.refs_1_), channel_id=1, source_target_pairs={{0,6},{1,7},{2,4},{3,5},{4,2},{5,3},{6,0},{7,1},{8,14},{9,15},{10,... | collective-permute-start | bytes 98312 | tf_op jit(solution)/shard_map/ppermute | solution.py:256
  72.1 4.3 %collective-permute-start.17 = (f32[8,1024]{1,0:T(8,128)S(1)}, f32[8,1024]{1,0:T(8,128)S(1)}, u32[]{:S(2)}, u32[]{:S(2)}) collective-permute-start(f32[8,1024]{1,0:T(8,128)S(1)} %get-tuple-element.51.refs_1_), channel_id=1, source_target_pairs={{0,2},{1,3},{2,0},{3,1},{4,6},{5,7},{6,4},{7,5},{8,10},{9,11},{10,... | collective-permute-start | bytes 98312 | tf_op jit(solution)/shard_map/ppermute | solution.py:256
  72.1 4.8 %collective-permute-start.18 = (f32[8,1024]{1,0:T(8,128)S(1)}, f32[8,1024]{1,0:T(8,128)S(1)}, u32[]{:S(2)}, u32[]{:S(2)}) collective-permute-start(f32[8,1024]{1,0:T(8,128)S(1)} %get-tuple-element.51.refs_1_), channel_id=1, source_target_pairs={{0,4},{1,5},{2,6},{3,7},{4,0},{5,1},{6,2},{7,3},{8,12},{9,13},{10,... | collective-permute-start | bytes 98312 | tf_op jit(solution)/shard_map/ppermute | solution.py:256
  77.0 2.7 %collective-permute-start.20 = (f32[4,8,1024]{2,1,0:T(8,128)S(1)}, f32[4,8,1024]{2,1,0:T(8,128)S(1)}, u32[]{:S(2)}, u32[]{:S(2)}) collective-permute-start(f32[4,8,1024]{2,1,0:T(8,128)S(1)} %pad_maximum_fusion.3.wa_ref), channel_id=1, source_target_pairs={{0,1},{1,0},{2,3},{3,2},{4,5},{5,4},{6,7},{7,6},{8,9},{9,8},{10,11... | collective-permute-start | bytes 393224 | tf_op jit(solution)/shard_map/ppermute | solution.py:256
  83.4 4.4 %collective-permute-start.22 = (f32[2,8,128]{2,1,0:T(8,128)S(1)}, f32[2,8,128]{2,1,0:T(8,128)S(1)}, u32[]{:S(2)}, u32[]{:S(2)}) collective-permute-start(f32[2,8,128]{2,1,0:T(8,128)S(1)} %add.13.refs_0_), channel_id=1, source_target_pairs={{0,2},{1,3},{2,0},{3,1},{4,6},{5,7},{6,4},{7,5},{8,10},{9,11},{10,... | collective-permute-start | bytes 24584 | tf_op jit(solution)/shard_map/ppermute | solution.py:256
  85.4 4.6 %collective-permute-start.23 = (f32[2,8,128]{2,1,0:T(8,128)S(1)}, f32[2,8,128]{2,1,0:T(8,128)S(1)}, u32[]{:S(2)}, u32[]{:S(2)}) collective-permute-start(f32[2,8,128]{2,1,0:T(8,128)S(1)} %add.13.refs_0_), channel_id=1, source_target_pairs={{0,4},{1,5},{2,6},{3,7},{4,0},{5,1},{6,2},{7,3},{8,12},{9,13},{10,... | collective-permute-start | bytes 24584 | tf_op jit(solution)/shard_map/ppermute | solution.py:256
  85.8 5.4 %collective-permute-start.24 = (f32[2,8,128]{2,1,0:T(8,128)S(1)}, f32[2,8,128]{2,1,0:T(8,128)S(1)}, u32[]{:S(2)}, u32[]{:S(2)}) collective-permute-start(f32[2,8,128]{2,1,0:T(8,128)S(1)} %add.13.refs_0_), channel_id=1, source_target_pairs={{0,6},{1,7},{2,4},{3,5},{4,2},{5,3},{6,0},{7,1},{8,14},{9,15},{10,... | collective-permute-start | bytes 24584 | tf_op jit(solution)/shard_map/ppermute | solution.py:256
  91.4 7.7 %collective-permute-start.27 = (f32[8,1024]{1,0:T(8,128)S(1)}, f32[8,1024]{1,0:T(8,128)S(1)}, u32[]{:S(2)}, u32[]{:S(2)}) collective-permute-start(f32[8,1024]{1,0:T(8,128)S(1)} %next_state.3), channel_id=1, source_target_pairs={{0,28},{1,29},{2,30},{3,31},{4,24},{5,25},{6,26},{7,27},{8,20},{9,... | collective-permute-start | bytes 98312 | tf_op jit(solution)/shard_map/ppermute | solution.py:256
  93.1 7.6 %collective-permute-start.28 = (f32[8,1024]{1,0:T(8,128)S(1)}, f32[8,1024]{1,0:T(8,128)S(1)}, u32[]{:S(2)}, u32[]{:S(2)}) collective-permute-start(f32[8,1024]{1,0:T(8,128)S(1)} %next_state.3), channel_id=1, source_target_pairs={{0,30},{1,31},{2,28},{3,29},{4,26},{5,27},{6,24},{7,25},{8,22},{9,... | collective-permute-start | bytes 98312 | tf_op jit(solution)/shard_map/ppermute | solution.py:256
  95.5 5.2 %collective-permute-start.25 = (f32[8,1024]{1,0:T(8,128)S(1)}, f32[8,1024]{1,0:T(8,128)S(1)}, u32[]{:S(2)}, u32[]{:S(2)}) collective-permute-start(f32[8,1024]{1,0:T(8,128)S(1)} %next_state.3), channel_id=1, source_target_pairs={{0,24},{1,25},{2,26},{3,27},{4,28},{5,29},{6,30},{7,31},{8,16},{9,... | collective-permute-start | bytes 98312 | tf_op jit(solution)/shard_map/ppermute | solution.py:256
  97.0 5.7 %collective-permute-start.26 = (f32[8,1024]{1,0:T(8,128)S(1)}, f32[8,1024]{1,0:T(8,128)S(1)}, u32[]{:S(2)}, u32[]{:S(2)}) collective-permute-start(f32[8,1024]{1,0:T(8,128)S(1)} %next_state.3), channel_id=1, source_target_pairs={{0,26},{1,27},{2,24},{3,25},{4,30},{5,31},{6,28},{7,29},{8,18},{9,... | collective-permute-start | bytes 98312 | tf_op jit(solution)/shard_map/ppermute | solution.py:256
  102.7 2.5 %collective-permute-start.29 = (f32[4,8,1024]{2,1,0:T(8,128)S(1)}, f32[4,8,1024]{2,1,0:T(8,128)S(1)}, u32[]{:S(2)}, u32[]{:S(2)}) collective-permute-start(f32[4,8,1024]{2,1,0:T(8,128)S(1)} %pad_maximum_fusion.4.xa_ref), channel_id=1, source_target_pairs={{0,1},{1,0},{2,3},{3,2},{4,5},{5,4},{6,7},{7,6},{8,9},{9,8},{10,11... | collective-permute-start | bytes 393224 | tf_op jit(solution)/shard_map/ppermute | solution.py:256
  107.5 5.9 %collective-permute-start.32 = (f32[8,1024]{1,0:T(8,128)S(1)}, f32[8,1024]{1,0:T(8,128)S(1)}, u32[]{:S(2)}, u32[]{:S(2)}) collective-permute-start(f32[8,1024]{1,0:T(8,128)S(1)} %get-tuple-element.59.refs_1_), channel_id=1, source_target_pairs={{0,6},{1,7},{2,4},{3,5},{4,2},{5,3},{6,0},{7,1},{8,14},{9,15},{10,... | collective-permute-start | bytes 98312 | tf_op jit(solution)/shard_map/ppermute | solution.py:256
  109.8 4.3 %collective-permute-start.30 = (f32[8,1024]{1,0:T(8,128)S(1)}, f32[8,1024]{1,0:T(8,128)S(1)}, u32[]{:S(2)}, u32[]{:S(2)}) collective-permute-start(f32[8,1024]{1,0:T(8,128)S(1)} %get-tuple-element.59.refs_1_), channel_id=1, source_target_pairs={{0,2},{1,3},{2,0},{3,1},{4,6},{5,7},{6,4},{7,5},{8,10},{9,11},{10,... | collective-permute-start | bytes 98312 | tf_op jit(solution)/shard_map/ppermute | solution.py:256
  109.8 4.8 %collective-permute-start.31 = (f32[8,1024]{1,0:T(8,128)S(1)}, f32[8,1024]{1,0:T(8,128)S(1)}, u32[]{:S(2)}, u32[]{:S(2)}) collective-permute-start(f32[8,1024]{1,0:T(8,128)S(1)} %get-tuple-element.59.refs_1_), channel_id=1, source_target_pairs={{0,4},{1,5},{2,6},{3,7},{4,0},{5,1},{6,2},{7,3},{8,12},{9,13},{10,... | collective-permute-start | bytes 98312 | tf_op jit(solution)/shard_map/ppermute | solution.py:256
  114.6 2.7 %collective-permute-start.33 = (f32[4,8,1024]{2,1,0:T(8,128)S(1)}, f32[4,8,1024]{2,1,0:T(8,128)S(1)}, u32[]{:S(2)}, u32[]{:S(2)}) collective-permute-start(f32[4,8,1024]{2,1,0:T(8,128)S(1)} %pad_maximum_fusion.5.wa_ref), channel_id=1, source_target_pairs={{0,1},{1,0},{2,3},{3,2},{4,5},{5,4},{6,7},{7,6},{8,9},{9,8},{10,11... | collective-permute-start | bytes 393224 | tf_op jit(solution)/shard_map/ppermute | solution.py:256
  121.3 4.4 %collective-permute-start.35 = (f32[2,8,128]{2,1,0:T(8,128)S(1)}, f32[2,8,128]{2,1,0:T(8,128)S(1)}, u32[]{:S(2)}, u32[]{:S(2)}) collective-permute-start(f32[2,8,128]{2,1,0:T(8,128)S(1)} %add.14.refs_0_), channel_id=1, source_target_pairs={{0,2},{1,3},{2,0},{3,1},{4,6},{5,7},{6,4},{7,5},{8,10},{9,11},{10,... | collective-permute-start | bytes 24584 | tf_op jit(solution)/shard_map/ppermute | solution.py:256
  123.3 4.5 %collective-permute-start.36 = (f32[2,8,128]{2,1,0:T(8,128)S(1)}, f32[2,8,128]{2,1,0:T(8,128)S(1)}, u32[]{:S(2)}, u32[]{:S(2)}) collective-permute-start(f32[2,8,128]{2,1,0:T(8,128)S(1)} %add.14.refs_0_), channel_id=1, source_target_pairs={{0,4},{1,5},{2,6},{3,7},{4,0},{5,1},{6,2},{7,3},{8,12},{9,13},{10,... | collective-permute-start | bytes 24584 | tf_op jit(solution)/shard_map/ppermute | solution.py:256
  124.0 5.4 %collective-permute-start.37 = (f32[2,8,128]{2,1,0:T(8,128)S(1)}, f32[2,8,128]{2,1,0:T(8,128)S(1)}, u32[]{:S(2)}, u32[]{:S(2)}) collective-permute-start(f32[2,8,128]{2,1,0:T(8,128)S(1)} %add.14.refs_0_), channel_id=1, source_target_pairs={{0,6},{1,7},{2,4},{3,5},{4,2},{5,3},{6,0},{7,1},{8,14},{9,15},{10,... | collective-permute-start | bytes 24584 | tf_op jit(solution)/shard_map/ppermute | solution.py:256
  129.6 5.9 %collective-permute-start.40 = (f32[8,1024]{1,0:T(8,128)S(1)}, f32[8,1024]{1,0:T(8,128)S(1)}, u32[]{:S(2)}, u32[]{:S(2)}) collective-permute-start(f32[8,1024]{1,0:T(8,128)S(1)} %next_state.4), channel_id=1, source_target_pairs={{0,12},{1,13},{2,14},{3,15},{4,8},{5,9},{6,10},{7,11},{8,4},{9,5},... | collective-permute-start | bytes 98312 | tf_op jit(solution)/shard_map/ppermute | solution.py:256
  130.9 6.6 %collective-permute-start.41 = (f32[8,1024]{1,0:T(8,128)S(1)}, f32[8,1024]{1,0:T(8,128)S(1)}, u32[]{:S(2)}, u32[]{:S(2)}) collective-permute-start(f32[8,1024]{1,0:T(8,128)S(1)} %next_state.4), channel_id=1, source_target_pairs={{0,14},{1,15},{2,12},{3,13},{4,10},{5,11},{6,8},{7,9},{8,6},{9,7},... | collective-permute-start | bytes 98312 | tf_op jit(solution)/shard_map/ppermute | solution.py:256
  132.4 5.1 %collective-permute-start.38 = (f32[8,1024]{1,0:T(8,128)S(1)}, f32[8,1024]{1,0:T(8,128)S(1)}, u32[]{:S(2)}, u32[]{:S(2)}) collective-permute-start(f32[8,1024]{1,0:T(8,128)S(1)} %next_state.4), channel_id=1, source_target_pairs={{0,8},{1,9},{2,10},{3,11},{4,12},{5,13},{6,14},{7,15},{8,0},{9,1},... | collective-permute-start | bytes 98312 | tf_op jit(solution)/shard_map/ppermute | solution.py:256
  133.9 4.8 %collective-permute-start.39 = (f32[8,1024]{1,0:T(8,128)S(1)}, f32[8,1024]{1,0:T(8,128)S(1)}, u32[]{:S(2)}, u32[]{:S(2)}) collective-permute-start(f32[8,1024]{1,0:T(8,128)S(1)} %next_state.4), channel_id=1, source_target_pairs={{0,10},{1,11},{2,8},{3,9},{4,14},{5,15},{6,12},{7,13},{8,2},{9,3},... | collective-permute-start | bytes 98312 | tf_op jit(solution)/shard_map/ppermute | solution.py:256
  138.7 2.5 %collective-permute-start.42 = (f32[4,8,1024]{2,1,0:T(8,128)S(1)}, f32[4,8,1024]{2,1,0:T(8,128)S(1)}, u32[]{:S(2)}, u32[]{:S(2)}) collective-permute-start(f32[4,8,1024]{2,1,0:T(8,128)S(1)} %pad_maximum_fusion.6.xa_ref), channel_id=1, source_target_pairs={{0,1},{1,0},{2,3},{3,2},{4,5},{5,4},{6,7},{7,6},{8,9},{9,8},{10,11... | collective-permute-start | bytes 393224 | tf_op jit(solution)/shard_map/ppermute | solution.py:256
  143.5 6.0 %collective-permute-start.45 = (f32[8,1024]{1,0:T(8,128)S(1)}, f32[8,1024]{1,0:T(8,128)S(1)}, u32[]{:S(2)}, u32[]{:S(2)}) collective-permute-start(f32[8,1024]{1,0:T(8,128)S(1)} %get-tuple-element.66.refs_1_), channel_id=1, source_target_pairs={{0,6},{1,7},{2,4},{3,5},{4,2},{5,3},{6,0},{7,1},{8,14},{9,15},{10,... | collective-permute-start | bytes 98312 | tf_op jit(solution)/shard_map/ppermute | solution.py:256
  145.8 4.4 %collective-permute-start.43 = (f32[8,1024]{1,0:T(8,128)S(1)}, f32[8,1024]{1,0:T(8,128)S(1)}, u32[]{:S(2)}, u32[]{:S(2)}) collective-permute-start(f32[8,1024]{1,0:T(8,128)S(1)} %get-tuple-element.66.refs_1_), channel_id=1, source_target_pairs={{0,2},{1,3},{2,0},{3,1},{4,6},{5,7},{6,4},{7,5},{8,10},{9,11},{10,... | collective-permute-start | bytes 98312 | tf_op jit(solution)/shard_map/ppermute | solution.py:256
  145.8 4.8 %collective-permute-start.44 = (f32[8,1024]{1,0:T(8,128)S(1)}, f32[8,1024]{1,0:T(8,128)S(1)}, u32[]{:S(2)}, u32[]{:S(2)}) collective-permute-start(f32[8,1024]{1,0:T(8,128)S(1)} %get-tuple-element.66.refs_1_), channel_id=1, source_target_pairs={{0,4},{1,5},{2,6},{3,7},{4,0},{5,1},{6,2},{7,3},{8,12},{9,13},{10,... | collective-permute-start | bytes 98312 | tf_op jit(solution)/shard_map/ppermute | solution.py:256
  150.6 2.7 %collective-permute-start.46 = (f32[4,8,1024]{2,1,0:T(8,128)S(1)}, f32[4,8,1024]{2,1,0:T(8,128)S(1)}, u32[]{:S(2)}, u32[]{:S(2)}) collective-permute-start(f32[4,8,1024]{2,1,0:T(8,128)S(1)} %pad_maximum_fusion.7.wa_ref), channel_id=1, source_target_pairs={{0,1},{1,0},{2,3},{3,2},{4,5},{5,4},{6,7},{7,6},{8,9},{9,8},{10,11... | collective-permute-start | bytes 393224 | tf_op jit(solution)/shard_map/ppermute | solution.py:256
  157.1 4.4 %collective-permute-start.48 = (f32[2,8,128]{2,1,0:T(8,128)S(1)}, f32[2,8,128]{2,1,0:T(8,128)S(1)}, u32[]{:S(2)}, u32[]{:S(2)}) collective-permute-start(f32[2,8,128]{2,1,0:T(8,128)S(1)} %add.15.refs_0_), channel_id=1, source_target_pairs={{0,2},{1,3},{2,0},{3,1},{4,6},{5,7},{6,4},{7,5},{8,10},{9,11},{10,... | collective-permute-start | bytes 24584 | tf_op jit(solution)/shard_map/ppermute | solution.py:256
  159.1 4.5 %collective-permute-start.49 = (f32[2,8,128]{2,1,0:T(8,128)S(1)}, f32[2,8,128]{2,1,0:T(8,128)S(1)}, u32[]{:S(2)}, u32[]{:S(2)}) collective-permute-start(f32[2,8,128]{2,1,0:T(8,128)S(1)} %add.15.refs_0_), channel_id=1, source_target_pairs={{0,4},{1,5},{2,6},{3,7},{4,0},{5,1},{6,2},{7,3},{8,12},{9,13},{10,... | collective-permute-start | bytes 24584 | tf_op jit(solution)/shard_map/ppermute | solution.py:256
  160.0 5.4 %collective-permute-start.50 = (f32[2,8,128]{2,1,0:T(8,128)S(1)}, f32[2,8,128]{2,1,0:T(8,128)S(1)}, u32[]{:S(2)}, u32[]{:S(2)}) collective-permute-start(f32[2,8,128]{2,1,0:T(8,128)S(1)} %add.15.refs_0_), channel_id=1, source_target_pairs={{0,6},{1,7},{2,4},{3,5},{4,2},{5,3},{6,0},{7,1},{8,14},{9,15},{10,... | collective-permute-start | bytes 24584 | tf_op jit(solution)/shard_map/ppermute | solution.py:256
  (4 other events, 5.4 us)
